TPU v7x, 128 devices: a whole 4x4x4 slice. The times are simulated.
128 devices in a mesh: ang: 8 (over z_lo, x), rad: 16 (over y, z_hi, core).
Axes of the slice: x: 4, y: 4, z: 4 (z_hi: 2, z_lo: 2; z = z_hi * 2 + z_lo), core: 2. Of those that a mesh axis runs over, the one named last changes fastest.
Arguments:
- right_side: float32 [2048, 8192], P('rad', 'ang'), may hold values from -6 to 7
- guess: float32 [2048, 8192], P('rad', 'ang'), may hold values from -6 to 6
Outputs:
- solution: float32 [2048, 8192], P('rad', 'ang')
- residual: float32 [2048, 8192], P('rad', 'ang')
All inputs are finite; a program needn't handle non-finite values.
Results may differ from a plain program's by a relative error of at most 0.007.
Values sent between devices are 32-bit elements; how exact they have to be, the bound alone decides.
A program may use at most 128 MiB of HBM per device.

v0:
```python
import math

import jax
import jax.numpy as jnp
from jax import lax
from jax.sharding import PartitionSpec as P

LEVELS = 8
PRE = 2
POST = 2
COARSE_SWEEPS = 8


def padded_2(x, sides, width, wrap):
    for axis, dim in sides:
        size, length = (lax.axis_size(axis), x.shape[dim])
        up = [(i, (i + 1) % size) for i in range(size if wrap else size - 1)]
        down = [(j, i) for i, j in up]
        last = lax.slice_in_dim(x, length - width, length, axis=dim)
        leading = lax.slice_in_dim(x, 0, width, axis=dim)
        before = lax.ppermute(last, axis, up)
        after = lax.ppermute(leading, axis, down)
        x = jnp.concatenate([before, x, after], axis=dim)
    return x


def joined_along(pieces, dim):
    pieces = jnp.moveaxis(pieces, 0, dim)
    shape = pieces.shape
    return pieces.reshape(*shape[:dim], shape[dim] * shape[dim + 1], *shape[dim + 2 :])


def from_everyone(x, axis):
    length = lax.axis_size(axis)
    return lax.all_to_all(jnp.broadcast_to(x[None], (length, *x.shape)), axis, 0, 0, tiled=True)


def gathered_copies(x, axis, dim):
    return joined_along(from_everyone(x, axis), dim)


def coefficients(row_float, spacing):
    radius = 1.0 + (row_float + 0.5) * spacing
    offset_ratio = 0.5 * spacing / radius
    outward = 1.0 + offset_ratio
    inward = 1.0 - offset_ratio
    angular = 1.0 / (radius * radius)
    centre = 2.0 + 2.0 * angular
    return (outward, inward, angular, centre)


def relax_cells(padded, source, stencil, chosen):
    outward, inward, angular, centre = stencil
    middle = padded[1:-1, 1:-1]
    updated = (
        source
        + outward * padded[2:, 1:-1]
        + inward * padded[:-2, 1:-1]
        + angular * (padded[1:-1, 2:] + padded[1:-1, :-2])
    ) / centre
    return jnp.where(chosen, updated, middle)


def apply_operator(padded, stencil):
    outward, inward, angular, centre = stencil
    middle = padded[1:-1, 1:-1]
    return (
        centre * middle
        - outward * padded[2:, 1:-1]
        - inward * padded[:-2, 1:-1]
        - angular * (padded[1:-1, 2:] + padded[1:-1, :-2])
    )


def restrict_grid(padded):
    height = padded.shape[0] - 2
    breadth = padded.shape[1] - 2
    row_sum = (
        padded[0:height:2]
        + 3.0 * padded[1 : height + 1 : 2]
        + 3.0 * padded[2 : height + 2 : 2]
        + padded[3 : height + 3 : 2]
    ) * 0.125
    col_sum = (
        row_sum[:, 0:breadth:2]
        + 3.0 * row_sum[:, 1 : breadth + 1 : 2]
        + 3.0 * row_sum[:, 2 : breadth + 2 : 2]
        + row_sum[:, 3 : breadth + 3 : 2]
    ) * 0.125
    return 4.0 * col_sum


def prolong_grid(padded):
    centre_rep = jnp.repeat(padded[1:-1], 2, axis=0)
    below_rep = jnp.repeat(padded[:-2], 2, axis=0)
    above_rep = jnp.repeat(padded[2:], 2, axis=0)
    row_ids = jnp.arange(centre_rep.shape[0], dtype=jnp.int32)[:, None]
    stretched = 0.75 * centre_rep + 0.25 * jnp.where(row_ids % 2 == 0, below_rep, above_rep)
    mid_cols = jnp.repeat(stretched[:, 1:-1], 2, axis=1)
    left_cols = jnp.repeat(stretched[:, :-2], 2, axis=1)
    right_cols = jnp.repeat(stretched[:, 2:], 2, axis=1)
    col_ids = jnp.arange(mid_cols.shape[1], dtype=jnp.int32)[None, :]
    return 0.75 * mid_cols + 0.25 * jnp.where(col_ids % 2 == 0, left_cols, right_cols)


def wrap_pad(values, margin):
    values = jnp.pad(values, ((0, 0), (margin, margin)), mode="wrap")
    return jnp.pad(values, ((margin, margin), (0, 0)))


def cycle_local(level_at, iterate, source):
    height, breadth = source.shape
    spacing = 2.0 * math.pi / breadth
    row_ids = jnp.arange(height, dtype=jnp.int32)[:, None]
    col_ids = jnp.arange(breadth, dtype=jnp.int32)[None, :]
    stencil = coefficients(row_ids.astype(jnp.float32), spacing)
    red_cells = (row_ids + col_ids) % 2 == 0
    black_cells = jnp.logical_not(red_cells)

    def colour_sweep(values):
        values = relax_cells(wrap_pad(values, 1), source, stencil, red_cells)
        return relax_cells(wrap_pad(values, 1), source, stencil, black_cells)

    if level_at == LEVELS - 1:
        for _ in range(COARSE_SWEEPS):
            iterate = colour_sweep(iterate)
        return iterate
    for _ in range(PRE):
        iterate = colour_sweep(iterate)
    remainder = source - apply_operator(wrap_pad(iterate, 1), stencil)
    coarse_source = restrict_grid(wrap_pad(remainder, 1))
    correction = cycle_local(level_at + 1, jnp.zeros_like(coarse_source), coarse_source)
    iterate = iterate + prolong_grid(wrap_pad(correction, 1))
    for _ in range(POST):
        iterate = colour_sweep(iterate)
    return iterate


def extend_halo(values, margin):
    values = padded_2(values, (("ang", 1),), margin, True)
    return padded_2(values, (("rad", 0),), margin, False)


def block_grid(height, breadth, lead):
    row_start = lax.axis_index("rad") * height - lead
    col_start = lax.axis_index("ang") * breadth - lead
    row_ids = row_start + jnp.arange(height + 2 * lead, dtype=jnp.int32)[:, None]
    col_ids = col_start + jnp.arange(breadth + 2 * lead, dtype=jnp.int32)[None, :]
    spacing = 2.0 * math.pi / (breadth * lax.axis_size("ang"))
    stencil = coefficients(row_ids.astype(jnp.float32), spacing)
    red_cells = (row_ids + col_ids) % 2 == 0
    inside = jnp.logical_and(row_ids >= 0, row_ids < height * lax.axis_size("rad"))
    return (stencil, red_cells, inside)


def cycle_spread(level_at, iterate, source, gather_level, layers):
    height, breadth = source.shape
    stencil, red_cells, inside = block_grid(height, breadth, 0)
    black_cells = jnp.logical_not(red_cells)
    loop_stencil, loop_red, loop_inside = block_grid(height, breadth, 1)
    loop_chosen = jnp.logical_and(loop_red, loop_inside)
    loop_source = extend_halo(source, 1)

    def colour_sweep(values):
        loop_cells = relax_cells(extend_halo(values, 2), loop_source, loop_stencil, loop_chosen)
        return relax_cells(loop_cells, source, stencil, black_cells)

    for _ in range(PRE):
        iterate = colour_sweep(iterate)
    remainder = source - apply_operator(extend_halo(iterate, 1), stencil)
    coarse_source = restrict_grid(extend_halo(remainder, 1))
    if level_at + 1 == gather_level:
        coarse_height, coarse_breadth = coarse_source.shape
        whole_grid = gathered_copies(coarse_source, "ang", 1)
        whole_grid = gathered_copies(whole_grid, "rad", 0)
        whole_fix = cycle_local(level_at + 1, jnp.zeros_like(whole_grid), whole_grid)
        correction = lax.dynamic_slice(
            whole_fix,
            (lax.axis_index("rad") * coarse_height, lax.axis_index("ang") * coarse_breadth),
            (coarse_height, coarse_breadth),
        )
    else:
        correction = cycle_spread(
            level_at + 1, jnp.zeros_like(coarse_source), coarse_source, gather_level, layers
        )
    iterate = iterate + prolong_grid(extend_halo(correction, 1))
    for _ in range(POST):
        iterate = colour_sweep(iterate)
    return iterate


def local(right_side, guess):
    gather_level = 5
    layers = 2
    solution = cycle_spread(0, guess, right_side, gather_level, layers)
    height, breadth = right_side.shape
    stencil, red_cells, inside = block_grid(height, breadth, 0)
    residual = right_side - apply_operator(extend_halo(solution, 1), stencil)
    return (solution, residual)


def solution(mesh):
    placed = (P("rad", "ang"), P("rad", "ang"))
    return jax.shard_map(
        local,
        mesh=mesh,
        in_specs=placed,
        out_specs=(P("rad", "ang"), P("rad", "ang")),
        check_vma=False,
    )
```

profile of v0, /device:TPU:46, one launch (start us, length us, event | category | flops | bytes accessed | tf_op | source)
XLA Modules:
  0.0 763.5 jit_solution(17479162626286362320)
XLA Ops:
  99.3 6.0 collective-permute-start.19
  166.1 5.4 collective-permute-done.31
  199.3 6.0 collective-permute-start.39
  249.0 5.4 collective-permute-done.51
  279.1 6.0 collective-permute-start.59
  299.7 6.0 collective-permute-start.63
  322.7 5.4 collective-permute-done.71
  352.4 6.0 collective-permute-start.79
  371.5 6.0 collective-permute-start.83
  393.2 5.3 collective-permute-done.91
  422.7 6.0 collective-permute-start.99
  431.3 5.4 all-to-all-start
  441.9 8.1 %all-to-all-start.1 = ((f32[16,4,256]{2,1,0:T(4,128)}), f32[16,4,256]{2,1,0:T(4,128)S(1)}, u32[]{:S(2)}, u32[]{:S(2)}) async-start(f32[16,4,256]{2,1,0:T(4,128)} %broadcast_in_dim.319), calls=%async_computation.1 | async-start | bytes 131072 | tf_op jit(solution)/shard_map/all_to_all | solution.py:35
  450.1 6.1 all-to-all-done.1
  484.8 6.0 collective-permute-start.103
  505.6 5.4 collective-permute-done.107
  535.3 6.0 collective-permute-start.115
  556.5 5.4 collective-permute-done.119
  586.2 6.0 collective-permute-start.127
  607.5 5.4 collective-permute-done.131
  637.9 6.0 collective-permute-start.139
  659.8 5.4 collective-permute-done.143
  691.6 6.3 collective-permute-start.151
  719.1 5.4 collective-permute-done.155
  (1074 shorter events, 617.1 us)
Async XLA Ops:
  1.6 33.3 %collective-permute-start.4 = (f32[128,2]{1,0:T(8,128)S(1)}, f32[128,2]{1,0:T(8,128)S(1)}, u32[]{:S(2)}, u32[]{:S(2)}) collective-permute-start(f32[128,2]{1,0:T(8,128)S(1)} %get-tuple-element.63), channel_id=1, source_target_pairs={{0,16},{16,32},{32,48},{48,64},{64,80},{80,96},{96,112},{112,0},{1... | collective-permute-start | bytes 3080 | tf_op jit(solution)/shard_map/ppermute | solution.py:21
  1.7 33.3 %collective-permute-start.5 = (f32[128,2]{1,0:T(8,128)S(1)}, f32[128,2]{1,0:T(8,128)S(1)}, u32[]{:S(2)}, u32[]{:S(2)}) collective-permute-start(f32[128,2]{1,0:T(8,128)S(1)} %get-tuple-element.62), channel_id=1, source_target_pairs={{16,0},{32,16},{48,32},{64,48},{80,64},{96,80},{112,96},{0,112},{1... | collective-permute-start | bytes 3080 | tf_op jit(solution)/shard_map/ppermute | solution.py:22
  4.6 25.2 %collective-permute-start = (f32[128,1]{1,0:T(8,128)S(1)}, f32[128,1]{1,0:T(8,128)S(1)}, u32[]{:S(2)}, u32[]{:S(2)}) collective-permute-start(f32[128,1]{1,0:T(8,128)S(1)} %get-tuple-element.61), channel_id=1, source_target_pairs={{0,16},{16,32},{32,48},{48,64},{64,80},{80,96},{96,112},{112,0},{1... | collective-permute-start | bytes 1544 | tf_op jit(solution)/shard_map/ppermute | solution.py:21
  6.9 23.0 %collective-permute-start.1 = (f32[128,1]{1,0:T(8,128)S(1)}, f32[128,1]{1,0:T(8,128)S(1)}, u32[]{:S(2)}, u32[]{:S(2)}) collective-permute-start(f32[128,1]{1,0:T(8,128)S(1)} %get-tuple-element.60), channel_id=1, source_target_pairs={{16,0},{32,16},{48,32},{64,48},{80,64},{96,80},{112,96},{0,112},{1... | collective-permute-start | bytes 1544 | tf_op jit(solution)/shard_map/ppermute | solution.py:22
  7.5 123.8 %collective-permute-start.24 = (f32[64,2]{1,0:T(8,128)}, f32[64,2]{1,0:T(8,128)S(1)}, u32[]{:S(2)}, u32[]{:S(2)}) collective-permute-start(f32[64,2]{1,0:T(8,128)} %broadcast.2045), channel_id=1, source_target_pairs={{0,16},{16,32},{32,48},{48,64},{64,80},{80,96},{96,112},{112,0},{1... | collective-permute-start | bytes 1544 | tf_op jit(solution)/shard_map/ppermute | solution.py:21
  29.8 101.5 %collective-permute-start.25 = (f32[64,2]{1,0:T(8,128)}, f32[64,2]{1,0:T(8,128)}, u32[]{:S(2)}, u32[]{:S(2)}) collective-permute-start(f32[64,2]{1,0:T(8,128)} %broadcast.2045), channel_id=1, source_target_pairs={{16,0},{32,16},{48,32},{64,48},{80,64},{96,80},{112,96},{0,112},{1... | collective-permute-start | bytes 1544 | tf_op jit(solution)/shard_map/ppermute | solution.py:22
  30.5 166.8 %collective-permute-start.44 = (f32[32,2]{1,0:T(8,128)}, f32[32,2]{1,0:T(8,128)}, u32[]{:S(2)}, u32[]{:S(2)}) collective-permute-start(f32[32,2]{1,0:T(8,128)} %broadcast.2055), channel_id=1, source_target_pairs={{0,16},{16,32},{32,48},{48,64},{64,80},{80,96},{96,112},{112,0},{1... | collective-permute-start | bytes 776 | tf_op jit(solution)/shard_map/ppermute | solution.py:21
  106.1 93.3 %collective-permute-start.45 = (f32[32,2]{1,0:T(8,128)}, f32[32,2]{1,0:T(8,128)}, u32[]{:S(2)}, u32[]{:S(2)}) collective-permute-start(f32[32,2]{1,0:T(8,128)} %broadcast.2055), channel_id=1, source_target_pairs={{16,0},{32,16},{48,32},{64,48},{80,64},{96,80},{112,96},{0,112},{1... | collective-permute-start | bytes 776 | tf_op jit(solution)/shard_map/ppermute | solution.py:22
  107.3 171.8 %collective-permute-start.64 = (f32[16,2]{1,0:T(8,128)}, f32[16,2]{1,0:T(8,128)}, u32[]{:S(2)}, u32[]{:S(2)}) collective-permute-start(f32[16,2]{1,0:T(8,128)} %broadcast.2070), channel_id=1, source_target_pairs={{0,16},{16,32},{32,48},{48,64},{64,80},{80,96},{96,112},{112,0},{1... | collective-permute-start | bytes 392 | tf_op jit(solution)/shard_map/ppermute | solution.py:21
  139.7 8.9 %collective-permute-start.22 = (f32[1,514]{1,0:T(1,128)S(1)}, f32[1,514]{1,0:T(1,128)S(1)}, u32[]{:S(2)}, u32[]{:S(2)}) collective-permute-start(f32[1,514]{1,0:T(1,128)S(1)} %get-tuple-element.77), channel_id=1, source_target_pairs={{0,1},{1,2},{2,3},{3,4},{4,5},{5,6},{6,7},{7,8},{8,9},{9,10},{10,1... | collective-permute-start | bytes 6176 | tf_op jit(solution)/shard_map/ppermute | solution.py:21
  193.1 92.1 %collective-permute-start.65 = (f32[16,2]{1,0:T(8,128)}, f32[16,2]{1,0:T(8,128)S(1)}, u32[]{:S(2)}, u32[]{:S(2)}) collective-permute-start(f32[16,2]{1,0:T(8,128)} %broadcast.2070), channel_id=1, source_target_pairs={{16,0},{32,16},{48,32},{64,48},{80,64},{96,80},{112,96},{0,112},{1... | collective-permute-start | bytes 392 | tf_op jit(solution)/shard_map/ppermute | solution.py:22
  195.3 144.3 %collective-permute-start.84 = (f32[8,2]{1,0:T(8,128)S(1)}, f32[8,2]{1,0:T(8,128)S(1)}, u32[]{:S(2)}, u32[]{:S(2)}) collective-permute-start(f32[8,2]{1,0:T(8,128)S(1)} %broadcast.2087), channel_id=1, source_target_pairs={{0,16},{16,32},{32,48},{48,64},{64,80},{80,96},{96,112},{112,0},{1... | collective-permute-start | bytes 200 | tf_op jit(solution)/shard_map/ppermute | solution.py:21
  197.4 8.8 %collective-permute-start.38 = (f32[1,514]{1,0:T(1,128)S(1)}, f32[1,514]{1,0:T(1,128)S(1)}, u32[]{:S(2)}, u32[]{:S(2)}) collective-permute-start(f32[1,514]{1,0:T(1,128)S(1)} %get-tuple-element.83), channel_id=1, source_target_pairs={{0,1},{1,2},{2,3},{3,4},{4,5},{5,6},{6,7},{7,8},{8,9},{9,10},{10,1... | collective-permute-start | bytes 6176 | tf_op jit(solution)/shard_map/ppermute | solution.py:21
  222.3 8.8 %collective-permute-start.42 = (f32[1,258]{1,0:T(1,128)S(1)}, f32[1,258]{1,0:T(1,128)S(1)}, u32[]{:S(2)}, u32[]{:S(2)}) collective-permute-start(f32[1,258]{1,0:T(1,128)S(1)} %get-tuple-element.135), channel_id=1, source_target_pairs={{0,1},{1,2},{2,3},{3,4},{4,5},{5,6},{6,7},{7,8},{8,9},{9,10},{10,1... | collective-permute-start | bytes 3104 | tf_op jit(solution)/shard_map/ppermute | solution.py:21
  274.9 64.7 %collective-permute-start.85 = (f32[8,2]{1,0:T(8,128)S(1)}, f32[8,2]{1,0:T(8,128)S(1)}, u32[]{:S(2)}, u32[]{:S(2)}) collective-permute-start(f32[8,2]{1,0:T(8,128)S(1)} %broadcast.2087), channel_id=1, source_target_pairs={{16,0},{32,16},{48,32},{64,48},{80,64},{96,80},{112,96},{0,112},{1... | collective-permute-start | bytes 200 | tf_op jit(solution)/shard_map/ppermute | solution.py:22
  277.2 10.7 %collective-permute-start.58 = (f32[1,258]{1,0:T(1,128)S(1)}, f32[1,258]{1,0:T(1,128)S(1)}, u32[]{:S(2)}, u32[]{:S(2)}) collective-permute-start(f32[1,258]{1,0:T(1,128)S(1)} %get-tuple-element.141), channel_id=1, source_target_pairs={{0,1},{1,2},{2,3},{3,4},{4,5},{5,6},{6,7},{7,8},{8,9},{9,10},{10,1... | collective-permute-start | bytes 3104 | tf_op jit(solution)/shard_map/ppermute | solution.py:21
  279.1 8.8 %collective-permute-start.59 = (f32[1,258]{1,0:T(1,128)S(1)}, f32[1,258]{1,0:T(1,128)S(1)}, u32[]{:S(2)}, u32[]{:S(2)}) collective-permute-start(f32[1,258]{1,0:T(1,128)S(1)} %get-tuple-element.142), channel_id=1, source_target_pairs={{1,0},{2,1},{3,2},{4,3},{5,4},{6,5},{7,6},{8,7},{9,8},{10,9},{11,1... | collective-permute-start | bytes 3104 | tf_op jit(solution)/shard_map/ppermute | solution.py:22
  286.0 13.7 %collective-permute-start.66 = (f32[2,132]{1,0:T(2,128)S(1)}, f32[2,132]{1,0:T(2,128)S(1)}, u32[]{:S(2)}, u32[]{:S(2)}) collective-permute-start(f32[2,132]{1,0:T(2,128)S(1)} %get-tuple-element.175), channel_id=1, source_target_pairs={{1,0},{2,1},{3,2},{4,3},{5,4},{6,5},{7,6},{8,7},{9,8},{10,9},{11,1... | collective-permute-start | bytes 3176 | tf_op jit(solution)/shard_map/ppermute | solution.py:22
  293.2 12.5 %collective-permute-start.67 = (f32[2,132]{1,0:T(2,128)S(1)}, f32[2,132]{1,0:T(2,128)S(1)}, u32[]{:S(2)}, u32[]{:S(2)}) collective-permute-start(f32[2,132]{1,0:T(2,128)S(1)} %get-tuple-element.174), channel_id=1, source_target_pairs={{0,1},{1,2},{2,3},{3,4},{4,5},{5,6},{6,7},{7,8},{8,9},{9,10},{10,1... | collective-permute-start | bytes 3176 | tf_op jit(solution)/shard_map/ppermute | solution.py:21
  350.5 12.3 %collective-permute-start.78 = (f32[1,130]{1,0:T(1,128)S(1)}, f32[1,130]{1,0:T(1,128)S(1)}, u32[]{:S(2)}, u32[]{:S(2)}) collective-permute-start(f32[1,130]{1,0:T(1,128)S(1)} %get-tuple-element.201), channel_id=1, source_target_pairs={{0,1},{1,2},{2,3},{3,4},{4,5},{5,6},{6,7},{7,8},{8,9},{9,10},{10,1... | collective-permute-start | bytes 1568 | tf_op jit(solution)/shard_map/ppermute | solution.py:21
  352.4 10.4 %collective-permute-start.79 = (f32[1,130]{1,0:T(1,128)S(1)}, f32[1,130]{1,0:T(1,128)S(1)}, u32[]{:S(2)}, u32[]{:S(2)}) collective-permute-start(f32[1,130]{1,0:T(1,128)S(1)} %get-tuple-element.202), channel_id=1, source_target_pairs={{1,0},{2,1},{3,2},{4,3},{5,4},{6,5},{7,6},{8,7},{9,8},{10,9},{11,1... | collective-permute-start | bytes 1568 | tf_op jit(solution)/shard_map/ppermute | solution.py:22
  358.5 19.0 %collective-permute-start.86 = (f32[2,68]{1,0:T(2,128)S(1)}, f32[2,68]{1,0:T(2,128)S(1)}, u32[]{:S(2)}, u32[]{:S(2)}) collective-permute-start(f32[2,68]{1,0:T(2,128)S(1)} %get-tuple-element.292), channel_id=1, source_target_pairs={{1,0},{2,1},{3,2},{4,3},{5,4},{6,5},{7,6},{8,7},{9,8},{10,9},{11,1... | collective-permute-start | bytes 1640 | tf_op jit(solution)/shard_map/ppermute | solution.py:22
  360.4 17.1 %collective-permute-start.87 = (f32[2,68]{1,0:T(2,128)S(1)}, f32[2,68]{1,0:T(2,128)S(1)}, u32[]{:S(2)}, u32[]{:S(2)}) collective-permute-start(f32[2,68]{1,0:T(2,128)S(1)} %get-tuple-element.291), channel_id=1, source_target_pairs={{0,1},{1,2},{2,3},{3,4},{4,5},{5,6},{6,7},{7,8},{8,9},{9,10},{10,1... | collective-permute-start | bytes 1640 | tf_op jit(solution)/shard_map/ppermute | solution.py:21
  441.9 14.3 %all-to-all-start.1 = ((f32[16,4,256]{2,1,0:T(4,128)}), f32[16,4,256]{2,1,0:T(4,128)S(1)}, u32[]{:S(2)}, u32[]{:S(2)}) async-start(f32[16,4,256]{2,1,0:T(4,128)} %broadcast_in_dim.319), calls=%async_computation.1 | async-start | bytes 131072 | tf_op jit(solution)/shard_map/all_to_all | solution.py:35
  (244 other events, 2336.0 us)
where the time goes:
time: 775 us; the launch traced here: 764 us
  starting transfers between devices  354 us (46%)
  waiting for transfers between devices  281 us (36%)
  local copies, waits for them, and re-layouts  61.9 us (8%)
  other arithmetic  61.1 us (8%)
    ppermute x82, starting transfers between devices, padded_2(): after = lax.ppermute(leading, axis, down)  214 us
    ppermute x82, waiting for transfers between devices, padded_2(): before = lax.ppermute(last, axis, up)  173 us
    ppermute x82, starting transfers between devices, padded_2(): before = lax.ppermute(last, axis, up)  126 us
    ppermute x82, waiting for transfers between devices, padded_2(): after = lax.ppermute(leading, axis, down)  102 us
    select_n x72, other arithmetic, relax_cells(): return jnp.where(chosen, updated, middle)  19.4 us
  transfers between devices with their start and end apart: 166, of which 108 were waited for; matrix products, arithmetic and copies ran while one was open for 9% of the time, Pallas kernels for 0%

commit v1 on v0

v1 whole, which is shorter than its diff:
```python
import math

import jax
import jax.numpy as jnp
from jax import lax
from jax.experimental import pallas as pl
from jax.experimental.pallas import tpu as pltpu
from jax.sharding import PartitionSpec as P

MESH = pl.DeviceIdType.MESH
F32 = jnp.float32
NR, NT = 2048, 8192
NA, NB = 8, 16
OWN = ((128, 8), (64, 4), (32, 2), (16, 1))
HALO = (8, 40, 16, 16)
BASE = tuple(h + 8 for h in HALO)
ROWS = tuple(o[0] + 2 * b for o, b in zip(OWN, BASE))
WHOLE = ((128, 4), (64, 2), (32, 1), (16, 1))
WB = 8
DIRS = tuple((dr, da) for dr in (-1, 0, 1) for da in (-1, 0, 1) if dr or da)
SIDES = tuple(d for d in DIRS if not d[0])
ENDS = tuple(d for d in DIRS if not d[1])
CORNERS = tuple(d for d in DIRS if d[0] and d[1])
PER = (9, 9, 8, 8)


def blocks(start, count, per, step):
    if count <= per:
        for k in range(count):
            step(start + 8 * k)
        return
    assert count % per == 0

    def body(i, carry):
        for k in range(per):
            step(pl.multiple_of(start + 8 * k + i * (8 * per), 8))
        return carry

    lax.fori_loop(0, count // per, body, 0)


def ids():
    sub = lax.broadcasted_iota(jnp.int32, (8, 128), 0)
    lane = lax.broadcasted_iota(jnp.int32, (8, 128), 1)
    return sub, lane


def ring_shift(tiles, lane):
    n = len(tiles)
    one = [pltpu.roll(x, 1, 1) for x in tiles]
    back = [pltpu.roll(x, 127, 1) for x in tiles]
    if n == 1:
        return one, back
    left = [jnp.where(lane == 0, one[t - 1], one[t]) for t in range(n)]
    right = [jnp.where(lane == 127, back[(t + 1) % n], back[t]) for t in range(n)]
    return left, right


def pick(x, index):
    return jnp.take_along_axis(x, index, axis=1, mode="promise_in_bounds")


def fill_coefficients(c_ref, count, base, first_row, total_rows, cells):
    h = 2.0 * math.pi / cells
    sub, _ = ids()

    def step(p):
        row = first_row + (p - base) + sub
        inside = jnp.logical_and(row >= 0, row < total_rows)
        r = 1.0 + (row.astype(F32) + 0.5) * h
        rr = r * r
        q = jnp.where(inside, 0.5 / (rr + 1.0), 0.0)
        half = (0.5 * h) * r
        at = pl.ds(p, 8)
        c_ref[0, at, :] = (rr + half) * q
        c_ref[1, at, :] = (rr - half) * q
        c_ref[2, at, :] = q
        c_ref[3, at, :] = rr * q
        c_ref[4, at, :] = 2.0 + 2.0 / rr

    blocks(0, count, 4 if count % 4 == 0 else count if count < 4 else 2, step)


def relaxed(src, g, c_ref, p, n, lane):
    at, above, below = pl.ds(p, 8), pl.ds(p + 1, 8), pl.ds(p - 1, 8)
    x = [src[t, at, :] for t in range(n)]
    left, right = ring_shift(x, lane)
    oc, ic, ac = c_ref[0, at, :], c_ref[1, at, :], c_ref[2, at, :]
    new = [
        (g[t, at, :] + oc * src[t, above, :]) + (ic * src[t, below, :] + ac * (left[t] + right[t]))
        for t in range(n)
    ]
    return x, new


def half_sweep(src, dst, g, c_ref, start, count, n, colour, per):
    sub, lane = ids()
    chosen = (sub + lane) % 2 == colour

    def step(p):
        x, new = relaxed(src, g, c_ref, p, n, lane)
        for t in range(n):
            dst[t, pl.ds(p, 8), :] = jnp.where(chosen, new[t], x[t])

    blocks(start, count, per, step)


def residual_pass(src, dst, g, c_ref, start, count, n, per, out_tiles=None):
    _, lane = ids()

    def step(p):
        x, new = relaxed(src, g, c_ref, p, n, lane)
        c = c_ref[4, pl.ds(p, 8), :]
        for t in range(out_tiles or n):
            dst[t, pl.ds(p, 8), :] = c * (new[t] - x[t])

    blocks(start, count, per, step)


def restrict_pass(s, fine_base, n, dst, coarse_base, c_ref, start, count, pairs, per):
    sub, lane = ids()
    even = lane % 2 == 0
    perm = jnp.where(lane < 64, 2 * lane, 2 * lane - 127)
    lo, hi = start // 8, start // 8 + count

    def step(p):
        f = 2 * (p - coarse_base) + fine_base
        r = [
            (s[t, pl.ds(f - 1, 8, stride=2), :] + s[t, pl.ds(f + 2, 8, stride=2), :])
            + 3.0 * (s[t, pl.ds(f, 8, stride=2), :] + s[t, pl.ds(f + 1, 8, stride=2), :])
            for t in range(n)
        ]
        left, right = ring_shift(r, lane)
        m = [3.0 * r[t] + jnp.where(even, left[t], right[t]) for t in range(n)]
        scale = c_ref[3, pl.ds(p, 8), :] * 0.0625
        for k, (a, b) in enumerate(pairs):
            joined = jnp.where(even, m[a] + pltpu.roll(m[a], 127, 1), m[b] + pltpu.roll(m[b], 1, 1))
            dst[k, pl.ds(p, 8), :] = pick(joined, perm) * scale

    del lo, hi
    blocks(coarse_base + start, count, per, step)


def prolong_pass(e, coarse_base, nc, f, start, count, fine, fine_base, plan, per, sealed):
    sub, lane = ids()
    even = lane % 2 == 0
    half = lane // 2
    kinds = (half, half + 64, jnp.where(lane < 64, half, half + 64))

    def across(p):
        x = [e[t, pl.ds(p, 8), :] for t in range(nc)]
        left, right = ring_shift(x, lane)
        a = [0.75 * x[t] + 0.25 * left[t] for t in range(nc)]
        b = [0.75 * x[t] + 0.25 * right[t] for t in range(nc)]
        for t, (source, kind) in enumerate(plan):
            f[t, pl.ds(p - (coarse_base + start) + 8, 8), :] = jnp.where(
                even, pick(a[source], kinds[kind]), pick(b[source], kinds[kind])
            )

    blocks(coarse_base + start, count, per, across)
    if sealed:
        for t in range(len(plan)):
            f[t, pl.ds(0, 8), :] = jnp.zeros((8, 128), F32)
            f[t, pl.ds(8 + 8 * count, 8), :] = jnp.zeros((8, 128), F32)

    def along(p):
        q = 2 * (p - 8 + start) + fine_base
        for t in range(len(plan)):
            mid = 0.75 * f[t, pl.ds(p, 8), :]
            first, second = pl.ds(q, 8, stride=2), pl.ds(q + 1, 8, stride=2)
            fine[t, first, :] = fine[t, first, :] + (mid + 0.25 * f[t, pl.ds(p - 1, 8), :])
            fine[t, second, :] = fine[t, second, :] + (mid + 0.25 * f[t, pl.ds(p + 1, 8), :])

    blocks(8, count, per, along)


def zero_rows(ref, n, start, count):
    for t in range(n):
        for k in range(count):
            ref[t, pl.ds(start + 8 * k, 8), :] = jnp.zeros((8, 128), F32)


def kernel(
    right_hbm, guess_hbm, sol_hbm, res_hbm,
    s0, g0, b0, g1, a1, b1, g2, a2, b2, s3, b3,
    g4, a4, b4, g5, a5, b5, g6, a6, b6, g7, a7, b7,
    win, f_ref, c0, c1, c2, c3, c4, c5, c6, c7,
    pk0, rp0, rd0, rl1, rd1, bk0, br0, bp0, bd0, bs3, own4, slots, strip,
    load_sem, out_sem, send0, recv0, send1, recv1, sendb, recvb, sendc, recvc, senda, recva, sendg, recvg,
):
    me_a, me_r = lax.axis_index("ang"), lax.axis_index("rad")

    def device(dr, da):
        return {"ang": lax.rem(me_a + da + NA, NA), "rad": lax.rem(me_r + dr + NB, NB)}

    a0 = s0.at[0]
    raw = s0.at[1]
    loads = []
    for t in range(8):
        for k, src in ((0, guess_hbm), (1, right_hbm)):
            loads.append(pltpu.make_async_copy(
                src.at[:, pl.ds(128 * t, 128)], s0.at[k, t, pl.ds(BASE[0], 128), :], load_sem.at[k, t]))
    for copy in loads:
        copy.start()

    barrier = pltpu.get_barrier_semaphore()
    partners = list(DIRS) + [(0, d) for d in range(2, NA - 1)] + [(d, 0) for d in range(2, NB - 1)]
    for dr, da in partners:
        pl.semaphore_signal(barrier, inc=1, device_id=device(dr, da), device_id_type=MESH)

    zero = jnp.zeros((8, 128), F32)
    for ref, l in ((a0, 0), (g0, 0), (b0, 0), (g1, 1), (a1, 1), (b1, 1), (g2, 2), (a2, 2), (b2, 2)):
        for t in range(OWN[l][1] + 1):
            ref[t, pl.ds(0, 8), :] = zero
            ref[t, pl.ds(ROWS[l] - 8, 8), :] = zero
    for ref in (s3.at[0], s3.at[1], b3):
        zero_rows(ref, 2, 0, ROWS[3] // 8)
    for l, refs in enumerate(((g4, a4, b4), (g5, a5, b5), (g6, a6, b6), (g7, a7, b7))):
        for ref in refs:
            for t in range(WHOLE[l][1]):
                ref[t, pl.ds(0, 8), :] = zero
                ref[t, pl.ds(WB + WHOLE[l][0], 8), :] = zero
    zero_rows(win, 1, 0, 5)

    def zf(i, carry):
        for t in range(9):
            f_ref[t, pl.ds(pl.multiple_of(8 * i, 8), 8), :] = zero
        return carry

    lax.fori_loop(0, 12, zf, 0)
    for l, c_ref in enumerate((c0, c1, c2, c3)):
        fill_coefficients(c_ref, ROWS[l] // 8, BASE[l], me_r * OWN[l][0], NR >> l, NT >> l)
    for l, c_ref in enumerate((c4, c5, c6, c7)):
        fill_coefficients(c_ref, WHOLE[l][0] // 8 + 2, WB, 0, WHOLE[l][0], NT >> (l + 4))

    sub, lane = ids()

    def pack(src, dst):
        for side, (tile, first) in enumerate(((0, 0), (7, 120))):
            total = None
            for b in range(16):
                x = src[tile, pl.ds(BASE[0] + 8 * b, 8), :]
                shift = (8 * b - first) % 128
                x = pltpu.roll(x, shift, 1) if shift else x
                total = x if total is None else jnp.where(lane // 8 == b, x, total)
            dst[side, :, :] = total

    def unpack(from_left, from_right, dst):
        for b in range(16):
            shift_r, shift_l = (-8 * b) % 128, (120 - 8 * b) % 128
            x = pltpu.roll(from_right, shift_r, 1) if shift_r else from_right
            y = pltpu.roll(from_left, shift_l, 1) if shift_l else from_left
            dst[8, pl.ds(BASE[0] + 8 * b, 8), :] = jnp.where(lane < 64, x, y)

    def remote(src, dst, sems, recvs, k, dr, da):
        return pltpu.make_async_remote_copy(
            src_ref=src, dst_ref=dst, send_sem=sems.at[k], recv_sem=recvs.at[k],
            device_id=device(dr, da), device_id_type=MESH)

    def edge(l, dr, width):
        if dr < 0:
            return pl.ds(BASE[l], width), pl.ds(BASE[l] + OWN[l][0], width)
        return pl.ds(BASE[l] + OWN[l][0] - width, width), pl.ds(BASE[l] - width, width)

    for copy in loads:
        copy.wait()
    for k in range(2):
        pack(s0.at[k], pk0.at[k])
    pl.semaphore_wait(barrier, len(partners))

    sends = []
    for k, (dr, da) in enumerate(DIRS):
        if da == 0:
            mine, theirs = edge(0, dr, 8)
            copy = remote(s0.at[:, pl.ds(0, 8), mine, :], s0.at[:, pl.ds(0, 8), theirs, :], send0, recv0, k, dr, da)
        elif dr == 0:
            side = 0 if da < 0 else 1
            copy = remote(pk0.at[:, side], rp0.at[:, side], send0, recv0, k, dr, da)
        else:
            mine, _ = edge(0, dr, 8)
            tile = 0 if da < 0 else 7
            copy = remote(s0.at[:, tile, mine, :], rd0.at[CORNERS.index((dr, da))], send0, recv0, k, dr, da)
        copy.start()
        sends.append(copy)

    def scale_own(p):
        w = c0[3, pl.ds(p, 8), :]
        for t in range(8):
            g0[t, pl.ds(p, 8), :] = raw[t, pl.ds(p, 8), :] * w

    blocks(BASE[0], 16, 8, scale_own)
    for copy in sends:
        copy.wait()

    def corners(dst, tile, buf, rows, l):
        for dr in (-1, 1):
            start = BASE[l] - rows if dr < 0 else BASE[l] + OWN[l][0]
            right = CORNERS.index((-dr, -1))
            left = CORNERS.index((-dr, 1))
            for j in range(rows // 8):
                x = buf(right)[pl.ds(8 * j, 8), :]
                y = buf(left)[pl.ds(8 * j, 8), :]
                dst[tile, pl.ds(start + 8 * j, 8), :] = jnp.where(lane < 64, x, y)

    for k in range(2):
        unpack(rp0[k, 1], rp0[k, 0], s0.at[k])
        corners(s0.at[k], 8, lambda c, k=k: rd0.at[c, k], 8, 0)

    def clear_outside(refs, l, n, depth):
        @pl.when(me_r == 0)
        def _():
            for ref in refs:
                zero_rows(ref, n, BASE[l] - depth, depth // 8)

        @pl.when(me_r == NB - 1)
        def _():
            for ref in refs:
                zero_rows(ref, n, BASE[l] + OWN[l][0], depth // 8)

    clear_outside((a0, raw), 0, 9, 8)
    for p in (8, BASE[0] + 128):
        w = c0[3, pl.ds(p, 8), :]
        for t in range(8):
            g0[t, pl.ds(p, 8), :] = raw[t, pl.ds(p, 8), :] * w

    def scale_tile(p):
        g0[8, pl.ds(p, 8), :] = raw[8, pl.ds(p, 8), :] * c0[3, pl.ds(p, 8), :]

    blocks(8, 18, 18, scale_tile)

    for colour, src, dst in ((0, a0, b0), (1, b0, a0), (0, a0, b0), (1, b0, a0)):
        half_sweep(src, dst, g0, c0, 8, 18, 9, colour, PER[0])
    residual_pass(a0, b0, g0, c0, 8, 18, 9, PER[0])
    restrict_pass(b0, BASE[0], 9, g1, BASE[1], c1, 0, 8, ((0, 1), (2, 3), (4, 5), (6, 7)), 4)

    sends = []
    for k, (dr, da) in enumerate(DIRS):
        tile = 0 if da < 0 else 3
        mine, theirs = edge(1, dr, 40) if dr else (pl.ds(BASE[1], 64), None)
        if da == 0:
            copy = remote(g1.at[pl.ds(0, 4), mine, :], g1.at[pl.ds(0, 4), theirs, :], send1, recv1, k, dr, da)
        elif dr == 0:
            copy = remote(g1.at[tile, mine, :], rl1.at[0 if da < 0 else 1], send1, recv1, k, dr, da)
        else:
            copy = remote(g1.at[tile, mine, :], rd1.at[CORNERS.index((dr, da))], send1, recv1, k, dr, da)
        copy.start()
        sends.append(copy)
    pack(a0, bk0)
    for copy in sends:
        copy.wait()

    back = []
    for k, (dr, da) in enumerate(DIRS):
        if da == 0:
            mine, _ = edge(0, dr, 8)
            copy = remote(a0.at[pl.ds(0, 8), mine, :], br0.at[0 if dr < 0 else 1], sendb, recvb, k, dr, da)
        elif dr == 0:
            side = 0 if da < 0 else 1
            copy = remote(bk0.at[side], bp0.at[side], sendb, recvb, k, dr, da)
        else:
            mine, _ = edge(0, dr, 8)
            copy = remote(a0.at[0 if da < 0 else 7, mine, :], bd0.at[CORNERS.index((dr, da))], sendb, recvb, k, dr, da)
        copy.start()
        back.append(copy)

    for b in range(8):
        g1[4, pl.ds(BASE[1] + 8 * b, 8), :] = jnp.where(
            lane < 64, rl1[0, pl.ds(8 * b, 8), :], rl1[1, pl.ds(8 * b, 8), :])
    corners(g1, 4, lambda c: rd1.at[c], 40, 1)
    clear_outside((g1,), 1, 5, 40)

    g3, a3 = s3.at[0], s3.at[1]

    def down(g, a, b, c, start, count, n, per):
        half_sweep(g, a, g, c, start, count, n, 1, per)
        half_sweep(a, b, g, c, start, count, n, 0, per)
        half_sweep(b, a, g, c, start, count, n, 1, per)
        residual_pass(a, b, g, c, start, count, n, per)

    down(g1, a1, b1, c1, 8, 18, 5, PER[1])
    restrict_pass(b1, BASE[1], 5, g2, BASE[2], c2, -16, 8, ((0, 1), (2, 3), (4, 4)), 8)
    down(g2, a2, b2, c2, BASE[2] - 16, 8, 3, PER[2])
    restrict_pass(b2, BASE[2], 3, g3, BASE[3], c3, -8, 4, ((0, 1), (2, 2)), 4)
    down(g3, a3, b3, c3, BASE[3] - 8, 4, 2, PER[3])

    sub, lane = ids()
    even = lane % 2 == 0
    r = [
        (b3[t, pl.ds(BASE[3] - 1, 8, stride=2), :] + b3[t, pl.ds(BASE[3] + 2, 8, stride=2), :])
        + 3.0 * (b3[t, pl.ds(BASE[3], 8, stride=2), :] + b3[t, pl.ds(BASE[3] + 1, 8, stride=2), :])
        for t in range(2)
    ]
    left, right = ring_shift(r, lane)
    m = 3.0 * r[0] + jnp.where(even, left[0], right[0])
    joined = jnp.where(even, m + pltpu.roll(m, 127, 1), m + pltpu.roll(m, 1, 1))
    perm = jnp.where(lane < 64, 2 * lane, 2 * lane - 127)
    my_rows = pl.ds(pl.multiple_of(WB + 8 * me_r, 8), 8)
    own4[...] = pick(joined, perm) * (c4[3, my_rows, :] * 0.0625)

    ring = []
    for d in range(1, NA):
        copy = remote(own4, slots.at[d - 1], senda, recva, d - 1, 0, d)
        copy.start()
        ring.append(copy)
    back3 = []
    for k, (dr, da) in enumerate(DIRS):
        copy = remote(s3.at[:, 0, pl.ds(BASE[3], 16), :], bs3.at[k], sendc, recvc, k, dr, da)
        copy.start()
        back3.append(copy)
    for copy in ring:
        copy.wait()
    for t in range(4):
        total = own4[...]
        for d in range(1, NA):
            source = lax.rem(me_a - d + NA, NA)
            hit = jnp.logical_and(source // 2 == t, lane // 64 == source % 2)
            total = jnp.where(hit, slots[d - 1], total)
        strip[t, :, :] = total
        g4[t, my_rows, :] = total
    column = []
    for d in range(1, NB):
        copy = remote(strip, g4.at[:, my_rows, :], sendg, recvg, d - 1, d, 0)
        copy.start()
        column.append(copy)
    for copy in column:
        copy.wait()

    def whole_down(g, a, b, c, l):
        down(g, a, b, c, WB, WHOLE[l][0] // 8, WHOLE[l][1], 16)

    def post(a, b, g, c, start, count, n, per):
        for colour, src, dst in ((0, a, b), (1, b, a), (0, a, b), (1, b, a)):
            half_sweep(src, dst, g, c, start, count, n, colour, per)

    whole_down(g4, a4, b4, c4, 0)
    restrict_pass(b4, WB, 4, g5, WB, c5, 0, 8, ((0, 1), (2, 3)), 8)
    whole_down(g5, a5, b5, c5, 1)
    restrict_pass(b5, WB, 2, g6, WB, c6, 0, 4, ((0, 1),), 4)
    whole_down(g6, a6, b6, c6, 2)
    restrict_pass(b6, WB, 1, g7, WB, c7, 0, 2, ((0, 0),), 2)
    half_sweep(g7, a7, g7, c7, WB, 2, 1, 1, 2)

    def coarse(i, carry):
        half_sweep(a7, b7, g7, c7, WB, 2, 1, 0, 2)
        half_sweep(b7, a7, g7, c7, WB, 2, 1, 1, 2)
        return carry

    lax.fori_loop(0, 7, coarse, 0)
    prolong_pass(a7, WB, 1, f_ref, 0, 2, a6, WB, ((0, 0),), 2, True)
    post(a6, b6, g6, c6, WB, 4, 1, 4)
    prolong_pass(a6, WB, 1, f_ref, 0, 4, a5, WB, ((0, 0), (0, 1)), 4, True)
    post(a5, b5, g5, c5, WB, 8, 2, 8)
    prolong_pass(a5, WB, 2, f_ref, 0, 8, a4, WB, ((0, 0), (0, 1), (1, 0), (1, 1)), 8, True)
    post(a4, b4, g4, c4, WB, 16, 4, 16)

    for k in range(3):
        rows = pl.ds(pl.multiple_of(WB + 8 * me_r, 8) + 8 * (k - 1), 8)

        def block(da, wanted):
            b = lax.rem(me_a + da + NA, NA)
            x = a4[b // 2, rows, :]
            return jnp.where(b % 2 == wanted, x, pltpu.roll(x, 64, 1))

        mine, rightward, leftward = block(0, 0), block(1, 1), block(-1, 1)
        win[0, pl.ds(8 + 8 * k, 8), :] = jnp.where(lane < 64, mine, jnp.where(lane < 96, rightward, leftward))

    for copy in back3:
        copy.wait()
    for q, ref in enumerate((g3, a3)):
        for half in range(2):
            at = pl.ds(8 * half, 8)
            got = lambda dr, da: bs3[DIRS.index((-dr, -da)), q, at, :]
            ref[0, pl.ds(BASE[3] - 16 + 8 * half, 8), :] = got(-1, 0)
            ref[0, pl.ds(BASE[3] + 16 + 8 * half, 8), :] = got(1, 0)
            for dr in (-1, 0, 1):
                ref[1, pl.ds(BASE[3] + 16 * dr + 8 * half, 8), :] = jnp.where(lane < 64, got(dr, 1), got(dr, -1))
    clear_outside((g3,), 3, 2, 16)
    prolong_pass(win, 16, 1, f_ref, -8, 3, a3, BASE[3], ((0, 0), (0, 1)), 3, False)
    clear_outside((a3,), 3, 2, 16)
    post(a3, b3, g3, c3, BASE[3] - 16, 6, 2, 6)

    prolong_pass(a3, BASE[3], 2, f_ref, -8, 4, a2, BASE[2], ((0, 0), (0, 1), (1, 2)), 4, False)
    clear_outside((a2,), 2, 3, 16)
    post(a2, b2, g2, c2, BASE[2] - 8, 6, 3, 6)

    prolong_pass(a2, BASE[2], 3, f_ref, -8, 6, a1, BASE[1], ((0, 0), (0, 1), (1, 0), (1, 1), (2, 2)), 6, False)
    clear_outside((a1,), 1, 5, 16)
    post(a1, b1, g1, c1, BASE[1] - 8, 10, 5, 10)

    for copy in back:
        copy.wait()
    unpack(bp0[1], bp0[0], a0)
    corners(a0, 8, lambda c: bd0.at[c], 8, 0)
    for t in range(8):
        a0[t, pl.ds(BASE[0] + 128, 8), :] = br0[0, t]
        a0[t, pl.ds(8, 8), :] = br0[1, t]
    plan = tuple((t // 2, t % 2) for t in range(8)) + ((4, 2),)
    prolong_pass(a1, BASE[1], 5, f_ref, -8, 10, a0, BASE[0], plan, 5, False)
    clear_outside((a0,), 0, 9, 16)
    post(a0, b0, g0, c0, 8, 18, 9, PER[0])

    outs = []
    for t in range(8):
        copy = pltpu.make_async_copy(
            a0.at[t, pl.ds(BASE[0], 128), :], sol_hbm.at[:, pl.ds(128 * t, 128)], out_sem.at[0, t])
        copy.start()
        outs.append(copy)
    residual_pass(a0, b0, g0, c0, BASE[0], 16, 9, 8, out_tiles=8)
    for t in range(8):
        copy = pltpu.make_async_copy(
            b0.at[t, pl.ds(BASE[0], 128), :], res_hbm.at[:, pl.ds(128 * t, 128)], out_sem.at[1, t])
        copy.start()
        outs.append(copy)
    for copy in outs:
        copy.wait()


def local(right_side, guess):
    def vm(*shape):
        return pltpu.VMEM(shape, F32)

    levels = [vm(2, 9, ROWS[0], 128), vm(9, ROWS[0], 128), vm(9, ROWS[0], 128)]
    for l in (1, 2):
        levels += [vm(OWN[l][1] + 1, ROWS[l], 128)] * 3
    levels += [vm(2, 2, ROWS[3], 128), vm(2, ROWS[3], 128)]
    for rows, tiles in WHOLE:
        levels += [vm(tiles, rows + 2 * WB, 128)] * 3
    coefficients = [vm(5, r, 128) for r in ROWS] + [vm(5, rows + 2 * WB, 128) for rows, _ in WHOLE]
    buffers = [
        vm(2, 2, 8, 128), vm(2, 2, 8, 128), vm(4, 2, 8, 128),
        vm(2, 64, 128), vm(4, 40, 128),
        vm(2, 8, 128), vm(2, 8, 8, 128), vm(2, 8, 128), vm(4, 8, 128),
        vm(8, 2, 16, 128), vm(8, 128), vm(NA - 1, 8, 128), vm(4, 8, 128),
    ]
    dma = pltpu.SemaphoreType.DMA
    sems = [dma((2, 8)), dma((2, 8))] + [dma((8,))] * 8 + [dma((NA - 1,))] * 2 + [dma((NB - 1,))] * 2
    block = jax.ShapeDtypeStruct(right_side.shape, F32)
    return pl.pallas_call(
        kernel,
        out_shape=(block, block),
        in_specs=[pl.BlockSpec(memory_space=pl.ANY)] * 2,
        out_specs=(pl.BlockSpec(memory_space=pl.ANY),) * 2,
        scratch_shapes=levels + [vm(1, 40, 128), vm(9, 96, 128)] + coefficients + buffers + sems,
        compiler_params=pltpu.CompilerParams(collective_id=0, has_side_effects=True),
    )(right_side, guess)


def solution(mesh):
    placed = (P("rad", "ang"), P("rad", "ang"))
    return jax.shard_map(local, mesh=mesh, in_specs=placed, out_specs=placed, check_vma=False)
```

time: 775 us -> 50.6 us (0.07)
  the two profiles are of different devices: /device:TPU:46 before, /device:TPU:1 now
where the time goes in v1:
time: 50.6 us; the launch traced here: 50.4 us
  Pallas kernels  47.1 us (93%)
  local copies, waits for them, and re-layouts  2.74 us (5%)
  between operations  0.65 us (1%)
    pallas_call x1, Pallas kernels, local(): pl.pallas_call(kernel, out_shape=(block, block), in_specs=[pl.BlockSpec(m...  47.1 us
    unnamed x4, local copies, waits for them, and re-layouts  2.74 us

profile of v1, /device:TPU:1, one launch (start us, length us, event | category | flops | bytes accessed | tf_op | source)
XLA Modules:
  0.0 50.4 jit_solution(4385216130419359303)
XLA Ops:
  0.6 47.1 %shard_map.41 = (f32[128,1024]{1,0:T(8,128)}, f32[128,1024]{1,0:T(8,128)}) custom-call(f32[128,1024]{1,0:T(8,128)} %right_hbm.1, f32[128,1024]{1,0:T(8,128)} %guess_hbm.1), custom_call_target="tpu_custom_call" | custom-call | tf_op jit(solution)/shard_map/pallas_call | solution.py:538
  47.7 0.0 copy-start
  47.7 1.9 %copy.6 = f32[128,1024]{1,0:T(8,128)} copy(f32[128,1024]{1,0:T(8,128)} %get-tuple-element.4) | data formatting | bytes 1048576
  49.6 0.0 copy-done
  49.7 0.8 %copy.7 = f32[128,1024]{1,0:T(8,128)} copy(f32[128,1024]{1,0:T(8,128)S(1)} %copy-done) | data formatting | bytes 1048576
Async XLA Ops:
  47.7 2.0 %copy-start = (f32[128,1024]{1,0:T(8,128)S(1)}, f32[128,1024]{1,0:T(8,128)}, u32[]{:S(2)}) copy-start(f32[128,1024]{1,0:T(8,128)} %get-tuple-element.5) | copy-start | bytes 1572868

commit v2 on v1

v2 whole, which is shorter than its diff:
```python
import math

import jax
import jax.numpy as jnp
from jax import lax
from jax.experimental import pallas as pl
from jax.experimental.pallas import tpu as pltpu
from jax.sharding import PartitionSpec as P

MESH = pl.DeviceIdType.MESH
F32 = jnp.float32
NR, NT = 2048, 8192
NA, NB = 8, 16
OWN = ((64, 8), (32, 4), (16, 2), (8, 1))
BASE = (8, 24, 16, 16)
ROWS = tuple(o[0] + 2 * b for o, b in zip(OWN, BASE))
E0, E1 = 5, 18
WHOLE = ((64, 4), (32, 2), (16, 1), (8, 1))
WB = 8
DIRS = tuple((dr, da) for dr in (-1, 0, 1) for da in (-1, 0, 1) if dr or da)
CORNERS = tuple(d for d in DIRS if d[0] and d[1])
FB = 16


def grid_ids():
    sub = lax.broadcasted_iota(jnp.int32, (8, 128), 0)
    lane = lax.broadcasted_iota(jnp.int32, (8, 128), 1)
    return sub, lane


def ring_shift(tiles, lane):
    n = len(tiles)
    one = [pltpu.roll(x, 1, 1) for x in tiles]
    back = [pltpu.roll(x, 127, 1) for x in tiles]
    if n == 1:
        return one, back
    left = [jnp.where(lane == 0, one[t - 1], one[t]) for t in range(n)]
    right = [jnp.where(lane == 127, back[(t + 1) % n], back[t]) for t in range(n)]
    return left, right


def pick(x, index):
    return jnp.take_along_axis(x, index, axis=1, mode="promise_in_bounds")


def fill_coefficients(c_ref, count, base, first_row, total_rows, cells):
    h = 2.0 * math.pi / cells
    sub, lane = grid_ids()
    even = lane % 2 == 0

    def row_values(row):
        inside = jnp.logical_and(row >= 0, row < total_rows)
        r = 1.0 + (row.astype(F32) + 0.5) * h
        rr = r * r
        q = jnp.where(inside, 0.5 / (rr + 1.0), 0.0)
        half = (0.5 * h) * r
        return (rr + half) * q, (rr - half) * q, q, rr * q, 2.0 + 2.0 / rr

    for k in range(count):
        row = first_row + 2 * (8 * k - base + sub)
        o0, i0, a0, w0, c0 = row_values(row)
        o1, i1, a1, w1, c1 = row_values(row + 1)
        at = pl.ds(8 * k, 8)
        for j, (x, y) in enumerate(((o0, i1), (i0, o1), (a0, a1), (w0, w1), (c0, c1))):
            c_ref[j, at, :] = jnp.where(even, x, y)
            c_ref[5 + j, at, :] = jnp.where(even, y, x)


def relaxed(src, g, c_ref, colour, p, n, lane):
    at = pl.ds(p, 8)
    even = lane % 2 == 0
    first, second = (p - 1, p + 1) if colour == 0 else (p + 1, p - 1)
    x = [src[t, at, :] for t in range(n)]
    left, right = ring_shift(x, lane)
    near, far, ang = (c_ref[5 * colour + k, at, :] for k in range(3))
    return [
        (g[t, at, :] + near * x[t])
        + (far * jnp.where(even, src[t, pl.ds(first, 8), :], src[t, pl.ds(second, 8), :]) + ang * (left[t] + right[t]))
        for t in range(n)
    ]


def half_sweep(dst, src, g, c_ref, colour, start, count, n):
    _, lane = grid_ids()
    for k in range(count):
        p = start + 8 * k
        new = relaxed(src, g, c_ref, colour, p, n, lane)
        for t in range(n):
            dst[t, pl.ds(p, 8), :] = new[t]


def residual_pass(dst, old, src, g, c_ref, colour, start, count, n, out_tiles=None):
    _, lane = grid_ids()
    for k in range(count):
        p = start + 8 * k
        new = relaxed(src, g, c_ref, colour, p, n, lane)
        c = c_ref[5 * colour + 4, pl.ds(p, 8), :]
        for t in range(out_tiles or n):
            dst[t, pl.ds(p, 8), :] = c * (new[t] - old[t, pl.ds(p, 8), :])


def restricted_block(s, p, n, pairs, lane):
    even = lane % 2 == 0
    perm = jnp.where(lane < 64, 2 * lane, 2 * lane - 127)
    r = [
        3.0 * s[t, pl.ds(p, 8), :] + jnp.where(even, s[t, pl.ds(p + 1, 8), :], s[t, pl.ds(p - 1, 8), :])
        for t in range(n)
    ]
    left, right = ring_shift(r, lane)
    m = [3.0 * r[t] + jnp.where(even, left[t], right[t]) for t in range(n)]
    out = []
    for a, b in pairs:
        joined = jnp.where(even, m[a] + pltpu.roll(m[a], 127, 1), m[b] + pltpu.roll(m[b], 1, 1))
        out.append(pick(joined, perm) * 0.0625)
    return out


def restrict_pass(s, fine_base, n, nat, g, coarse_base, c_ref, start, count, pairs):
    _, lane = grid_ids()
    even = lane % 2 == 0
    for k in range(2 * count):
        for t, x in enumerate(restricted_block(s, fine_base + 2 * start + 8 * k, n, pairs, lane)):
            nat[t, pl.ds(8 * k, 8), :] = x
    for k in range(count):
        p = pl.ds(coarse_base + start + 8 * k, 8)
        red, black = c_ref[3, p, :], c_ref[8, p, :]
        for t in range(len(pairs)):
            x = nat[t, pl.ds(16 * k, 8, stride=2), :]
            y = nat[t, pl.ds(16 * k + 1, 8, stride=2), :]
            g[0, t, p, :] = jnp.where(even, x, y) * red
            g[1, t, p, :] = jnp.where(even, y, x) * black


def unpair(red, black, p, dst, q, n):
    _, lane = grid_ids()
    even = lane % 2 == 0
    for t in range(n):
        x, y = red[t, pl.ds(p, 8), :], black[t, pl.ds(p, 8), :]
        dst[t, pl.ds(q, 8, stride=2), :] = jnp.where(even, x, y)
        dst[t, pl.ds(q + 1, 8, stride=2), :] = jnp.where(even, y, x)


def prolong_pass(e, f, start, count, fine, fine_base, fine_start, fine_count, plan, sealed):
    _, lane = grid_ids()
    even = lane % 2 == 0
    half = lane // 2
    kinds = (half, half + 64, jnp.where(lane < 64, half, half + 64))
    nc = max(source for source, _ in plan) + 1
    for k in range(count):
        p = FB + start + 8 * k
        x = [e[t, pl.ds(p, 8), :] for t in range(nc)]
        left, right = ring_shift(x, lane)
        a = [0.75 * x[t] + 0.25 * left[t] for t in range(nc)]
        b = [0.75 * x[t] + 0.25 * right[t] for t in range(nc)]
        for t, (source, kind) in enumerate(plan):
            f[t, pl.ds(p, 8), :] = jnp.where(even, pick(a[source], kinds[kind]), pick(b[source], kinds[kind]))
    if sealed:
        for t in range(len(plan)):
            f[t, pl.ds(FB - 8, 8), :] = jnp.zeros((8, 128), F32)
            f[t, pl.ds(FB + 8 * count, 8), :] = jnp.zeros((8, 128), F32)
    for k in range(fine_count):
        i = fine_start + 8 * k
        at = pl.ds(fine_base + i, 8)
        for t in range(len(plan)):
            other = jnp.where(even, f[t, pl.ds(FB + i + 1, 8), :], f[t, pl.ds(FB + i - 1, 8), :])
            fine[t, at, :] = fine[t, at, :] + (0.75 * f[t, pl.ds(FB + i, 8), :] + 0.25 * other)


def zero_rows(ref, n, start, count):
    for t in range(n):
        for k in range(count):
            ref[t, pl.ds(start + 8 * k, 8), :] = jnp.zeros((8, 128), F32)


def down(r, k, g, s, c, start, count, n):
    half_sweep(k, g.at[0], g.at[1], c, 1, start, count, n)
    half_sweep(r, k, g.at[0], c, 0, start, count, n)
    half_sweep(k, r, g.at[1], c, 1, start, count, n)
    residual_pass(s, r, k, g.at[0], c, 0, start, count, n)


def post(r, k, g, c, start, count, n):
    for _ in range(2):
        half_sweep(r, k, g.at[0], c, 0, start, count, n)
        half_sweep(k, r, g.at[1], c, 1, start, count, n)


def kernel(
    right_hbm, guess_hbm, sol_hbm, res_hbm,
    raw, x0, r0, s0, g1, r1, k1, s1, g2, r2, k2, s2, x3, r3, s3,
    g4, r4, k4, s4, g5, r5, k5, s5, g6, r6, k6, s6, g7, r7, k7,
    win, e_ref, f_ref, nat, c0, c1, c2, c3, c4, c5, c6, c7,
    pk0, rp0, rd0, rl1, rd1, bs3, own4, slots, strip,
    load_sem, out_sem, send0, recv0, send1, recv1, sendc, recvc, senda, recva, sendg, recvg,
):
    me_a, me_r = lax.axis_index("ang"), lax.axis_index("rad")

    def device(dr, da):
        return {"ang": lax.rem(me_a + da + NA, NA), "rad": lax.rem(me_r + dr + NB, NB)}

    loads = []
    for t in range(8):
        for k, src in ((0, guess_hbm), (1, right_hbm)):
            loads.append(pltpu.make_async_copy(
                src.at[:, pl.ds(128 * t, 128)], raw.at[k, t], load_sem.at[k, t]))
    for copy in loads:
        copy.start()

    barrier = pltpu.get_barrier_semaphore()
    partners = list(DIRS) + [(0, d) for d in range(2, NA - 1)] + [(d, 0) for d in range(2, NB - 1)]
    for dr, da in partners:
        pl.semaphore_signal(barrier, inc=1, device_id=device(dr, da), device_id_type=MESH)

    zero = jnp.zeros((8, 128), F32)
    k0, g0 = x0.at[0], x0.at[pl.ds(1, 2)]
    k3, g3 = x3.at[0], x3.at[pl.ds(1, 2)]
    edges = [(r, 0) for r in (r0, s0)] + [(r, 1) for r in (r1, k1, s1)]
    edges += [(r, 2) for r in (g2.at[0], g2.at[1], r2, k2, s2)]
    edges += [(r, 3) for r in (k3, x3.at[1], x3.at[2], r3, s3)]
    for ref, l in edges:
        depth = 1 if l < 2 else 2
        for t in range(OWN[l][1] + 1):
            for d in range(depth):
                ref[t, pl.ds(8 * d, 8), :] = zero
                ref[t, pl.ds(ROWS[l] - 8 - 8 * d, 8), :] = zero
    for l, refs in enumerate(((g4, r4, k4, s4), (g5, r5, k5, s5), (g6, r6, k6, s6), (g7, r7, k7))):
        for ref in refs:
            for x in ((ref.at[0], ref.at[1]) if len(ref.shape) == 4 else (ref,)):
                for t in range(WHOLE[l][1]):
                    x[t, pl.ds(0, 8), :] = zero
                    x[t, pl.ds(WB + WHOLE[l][0], 8), :] = zero
    zero_rows(win, 1, 0, 6)
    for t in range(9):
        for d in (0, 1, 10, 11):
            f_ref[t, pl.ds(8 * d, 8), :] = zero
    for l, c_ref in enumerate((c0, c1, c2, c3)):
        fill_coefficients(c_ref, ROWS[l] // 8, BASE[l], me_r * (2 * OWN[l][0]), NR >> l, NT >> l)
    for l, c_ref in enumerate((c4, c5, c6, c7)):
        fill_coefficients(c_ref, WHOLE[l][0] // 8 + 2, WB, 0, 2 * WHOLE[l][0], NT >> (l + 4))

    sub, lane = grid_ids()
    even = lane % 2 == 0

    def remote(src, dst, sems, recvs, k, dr, da):
        return pltpu.make_async_remote_copy(
            src_ref=src, dst_ref=dst, send_sem=sems.at[k], recv_sem=recvs.at[k],
            device_id=device(dr, da), device_id_type=MESH)

    def edge(l, dr, width):
        if dr < 0:
            return pl.ds(BASE[l], width), pl.ds(BASE[l] + OWN[l][0], width)
        return pl.ds(BASE[l] + OWN[l][0] - width, width), pl.ds(BASE[l] - width, width)

    for copy in loads:
        copy.wait()
    for k in range(8):
        at = pl.ds(BASE[0] + 8 * k, 8)
        red, black = c0[3, at, :], c0[8, at, :]
        for t in range(8):
            k0[t, at, :] = jnp.where(
                even, raw[0, t, pl.ds(16 * k + 1, 8, stride=2), :], raw[0, t, pl.ds(16 * k, 8, stride=2), :])
            x = raw[1, t, pl.ds(16 * k, 8, stride=2), :]
            y = raw[1, t, pl.ds(16 * k + 1, 8, stride=2), :]
            g0[0, t, at, :] = jnp.where(even, x, y) * red
            g0[1, t, at, :] = jnp.where(even, y, x) * black
    for q in range(3):
        for side, (tile, first) in enumerate(((0, 0), (7, 112))):
            total = None
            for b in range(8):
                x = x0[q, tile, pl.ds(BASE[0] + 8 * b, 8), :]
                shift = (16 * b - first) % 128
                x = pltpu.roll(x, shift, 1) if shift else x
                total = x if total is None else jnp.where(lane // 16 == b, x, total)
            pk0[side, q, :, :] = total
    pl.semaphore_wait(barrier, len(partners))

    sends = []
    for k, (dr, da) in enumerate(DIRS):
        if da == 0:
            mine, theirs = edge(0, dr, E0)
            copy = remote(x0.at[:, pl.ds(0, 8), mine, :], x0.at[:, pl.ds(0, 8), theirs, :], send0, recv0, k, dr, da)
        elif dr == 0:
            side = 0 if da < 0 else 1
            copy = remote(pk0.at[side], rp0.at[side], send0, recv0, k, dr, da)
        else:
            mine, _ = edge(0, dr, E0)
            tile = 0 if da < 0 else 7
            copy = remote(
                x0.at[:, tile, mine, :], rd0.at[CORNERS.index((dr, da)), :, pl.ds(0, E0), :], send0, recv0, k, dr, da)
        copy.start()
        sends.append(copy)
    for copy in sends:
        copy.wait()

    def clear_outside(refs, l, n, depth=1):
        @pl.when(me_r == 0)
        def _():
            for ref in refs:
                zero_rows(ref, n, BASE[l] - 8 * depth, depth)

        @pl.when(me_r == NB - 1)
        def _():
            for ref in refs:
                zero_rows(ref, n, BASE[l] + OWN[l][0], depth)

    for q in range(3):
        from_left, from_right = rp0[1, q], rp0[0, q]
        for b in range(8):
            shift_r, shift_l = (-16 * b) % 128, (112 - 16 * b) % 128
            x = pltpu.roll(from_right, shift_r, 1) if shift_r else from_right
            y = pltpu.roll(from_left, shift_l, 1) if shift_l else from_left
            x0[q, 8, pl.ds(BASE[0] + 8 * b, 8), :] = jnp.where(lane < 64, x, y)
        for dr in (-1, 1):
            start = BASE[0] - E0 if dr < 0 else BASE[0] + OWN[0][0]
            x = rd0[CORNERS.index((-dr, -1)), q, pl.ds(0, E0), :]
            y = rd0[CORNERS.index((-dr, 1)), q, pl.ds(0, E0), :]
            x0[q, 8, pl.ds(start, E0), :] = jnp.where(lane[:E0] < 64, x, y)
    clear_outside((k0, g0.at[0], g0.at[1]), 0, 9)

    for _ in range(2):
        half_sweep(r0, k0, g0.at[0], c0, 0, 4, 9, 9)
        half_sweep(k0, r0, g0.at[1], c0, 1, 4, 9, 9)
    residual_pass(s0, r0, k0, g0.at[0], c0, 0, 4, 9, 9)
    restrict_pass(s0, BASE[0], 9, nat, g1, BASE[1], c1, 0, 4, ((0, 1), (2, 3), (4, 5), (6, 7)))

    sends = []
    for k, (dr, da) in enumerate(DIRS):
        tile = 0 if da < 0 else 3
        mine, theirs = edge(1, dr, E1) if dr else (pl.ds(BASE[1], 32), None)
        if da == 0:
            copy = remote(g1.at[:, pl.ds(0, 4), mine, :], g1.at[:, pl.ds(0, 4), theirs, :], send1, recv1, k, dr, da)
        elif dr == 0:
            copy = remote(g1.at[:, tile, mine, :], rl1.at[0 if da < 0 else 1], send1, recv1, k, dr, da)
        else:
            copy = remote(
                g1.at[:, tile, mine, :], rd1.at[CORNERS.index((dr, da)), :, pl.ds(0, E1), :], send1, recv1, k, dr, da)
        copy.start()
        sends.append(copy)
    for copy in sends:
        copy.wait()
    for q in range(2):
        for b in range(4):
            g1[q, 4, pl.ds(BASE[1] + 8 * b, 8), :] = jnp.where(
                lane < 64, rl1[0, q, pl.ds(8 * b, 8), :], rl1[1, q, pl.ds(8 * b, 8), :])
        for dr in (-1, 1):
            start = BASE[1] - E1 if dr < 0 else BASE[1] + OWN[1][0]
            for first, size in ((0, 8), (8, 8), (16, 2)):
                x = rd1[CORNERS.index((-dr, -1)), q, pl.ds(first, size), :]
                y = rd1[CORNERS.index((-dr, 1)), q, pl.ds(first, size), :]
                g1[q, 4, pl.ds(start + first, size), :] = jnp.where(lane[:size] < 64, x, y)
            rest = BASE[1] - E1 - 3 if dr < 0 else BASE[1] + OWN[1][0] + E1
            for t in range(5):
                g1[q, t, pl.ds(rest, 3), :] = jnp.zeros((3, 128), F32)
    clear_outside((g1.at[0], g1.at[1]), 1, 5, 3)

    down(r1, k1, g1, s1, c1, BASE[1] - 20, 9, 5)
    restrict_pass(s1, BASE[1], 5, nat, g2, BASE[2], c2, -8, 4, ((0, 1), (2, 3), (4, 4)))
    down(r2, k2, g2, s2, c2, BASE[2] - 8, 4, 3)
    restrict_pass(s2, BASE[2], 3, nat, g3, BASE[3], c3, -4, 2, ((0, 1), (2, 2)))
    down(r3, k3, g3, s3, c3, BASE[3] - 4, 2, 2)

    nat[0, pl.ds(0, 8), :] = restricted_block(s3, BASE[3], 2, ((0, 0),), lane)[0]
    x, y = nat[0, pl.ds(0, 4, stride=2), :], nat[0, pl.ds(1, 4, stride=2), :]
    my_pairs = pl.ds(WB + 4 * me_r, 4)
    own4[pl.ds(0, 4), :] = jnp.where(even[:4], x, y) * c4[3, my_pairs, :]
    own4[pl.ds(4, 4), :] = jnp.where(even[:4], y, x) * c4[8, my_pairs, :]
    ring = []
    for d in range(1, NA):
        copy = remote(own4, slots.at[d - 1], senda, recva, d - 1, 0, d)
        copy.start()
        ring.append(copy)
    back3 = []
    for k, (dr, da) in enumerate(DIRS):
        copy = remote(x3.at[:, 0, pl.ds(BASE[3], 8), :], bs3.at[k], sendc, recvc, k, dr, da)
        copy.start()
        back3.append(copy)
    for copy in ring:
        copy.wait()
    for t in range(4):
        total = own4[...]
        for d in range(1, NA):
            source = lax.rem(me_a - d + NA, NA)
            hit = jnp.logical_and(source // 2 == t, lane // 64 == source % 2)
            total = jnp.where(hit, slots[d - 1], total)
        for q in range(2):
            strip[q, t, pl.ds(0, 4), :] = total[4 * q:4 * q + 4]
            g4[q, t, my_pairs, :] = total[4 * q:4 * q + 4]
    column = []
    for d in range(1, NB):
        copy = remote(strip.at[:, :, pl.ds(0, 4), :], g4.at[:, :, my_pairs, :], sendg, recvg, d - 1, d, 0)
        copy.start()
        column.append(copy)
    for copy in column:
        copy.wait()

    down(r4, k4, g4, s4, c4, WB, 8, 4)
    restrict_pass(s4, WB, 4, nat, g5, WB, c5, 0, 4, ((0, 1), (2, 3)))
    down(r5, k5, g5, s5, c5, WB, 4, 2)
    restrict_pass(s5, WB, 2, nat, g6, WB, c6, 0, 2, ((0, 1),))
    down(r6, k6, g6, s6, c6, WB, 2, 1)
    restrict_pass(s6, WB, 1, nat, g7, WB, c7, 0, 1, ((0, 0),))
    half_sweep(k7, g7.at[0], g7.at[1], c7, 1, WB, 1, 1)
    for _ in range(7):
        half_sweep(r7, k7, g7.at[0], c7, 0, WB, 1, 1)
        half_sweep(k7, r7, g7.at[1], c7, 1, WB, 1, 1)

    def whole_up(rc, kc, blocks, nc, fine, plan):
        for k in range(blocks):
            unpair(rc, kc, WB + 8 * k, e_ref, FB + 16 * k, nc)
        prolong_pass(e_ref, f_ref, 0, 2 * blocks, fine, WB, 0, 2 * blocks, plan, True)

    whole_up(r7, k7, 1, 1, k6, ((0, 0),))
    post(r6, k6, g6, c6, WB, 2, 1)
    whole_up(r6, k6, 2, 1, k5, ((0, 0), (0, 1)))
    post(r5, k5, g5, c5, WB, 4, 2)
    whole_up(r5, k5, 4, 2, k4, ((0, 0), (0, 1), (1, 0), (1, 1)))
    post(r4, k4, g4, c4, WB, 8, 4)

    def block(ref, da, wanted, at):
        b = lax.rem(me_a + da + NA, NA)
        x = ref[b // 2, at, :]
        return jnp.where(b % 2 == wanted, x, pltpu.roll(x, 64, 1))

    for k in range(2):
        at = pl.ds(WB - 4 + 4 * me_r + 8 * k, 8)
        seen = []
        for ref in (r4, k4):
            mine, rightward, leftward = block(ref, 0, 0, at), block(ref, 1, 1, at), block(ref, -1, 1, at)
            seen.append(jnp.where(lane < 64, mine, jnp.where(lane < 96, rightward, leftward)))
        q = FB - 8 + 16 * k
        win[0, pl.ds(q, 8, stride=2), :] = jnp.where(even, seen[0], seen[1])
        win[0, pl.ds(q + 1, 8, stride=2), :] = jnp.where(even, seen[1], seen[0])

    for copy in back3:
        copy.wait()
    for q in range(3):
        got = lambda dr, da: bs3[DIRS.index((-dr, -da)), q]
        x3[q, 0, pl.ds(BASE[3] - 8, 8), :] = got(-1, 0)
        x3[q, 0, pl.ds(BASE[3] + 8, 8), :] = got(1, 0)
        for dr in (-1, 0, 1):
            x3[q, 1, pl.ds(BASE[3] + 8 * dr, 8), :] = jnp.where(lane < 64, got(dr, 1), got(dr, -1))
    prolong_pass(win, f_ref, -8, 3, k3, BASE[3], -8, 3, ((0, 0), (0, 1)), False)
    clear_outside((k3, g3.at[0], g3.at[1]), 3, 2)
    post(r3, k3, g3, c3, BASE[3] - 8, 3, 2)

    for k in range(2):
        unpair(r3, k3, BASE[3] - 4 + 8 * k, e_ref, FB - 8 + 16 * k, 2)
    prolong_pass(e_ref, f_ref, -8, 4, k2, BASE[2], -4, 3, ((0, 0), (0, 1), (1, 2)), False)
    clear_outside((k2,), 2, 3)
    post(r2, k2, g2, c2, BASE[2] - 4, 3, 3)

    for k in range(3):
        unpair(r2, k2, BASE[2] - 4 + 8 * k, e_ref, FB - 8 + 16 * k, 3)
    prolong_pass(e_ref, f_ref, -8, 6, k1, BASE[1], -4, 5, ((0, 0), (0, 1), (1, 0), (1, 1), (2, 2)), False)
    clear_outside((k1,), 1, 5)
    post(r1, k1, g1, c1, BASE[1] - 4, 5, 5)

    for k in range(5):
        unpair(r1, k1, BASE[1] - 4 + 8 * k, e_ref, FB - 8 + 16 * k, 5)
    plan = tuple((t // 2, t % 2) for t in range(8)) + ((4, 2),)
    prolong_pass(e_ref, f_ref, -8, 10, k0, BASE[0], -4, 9, plan, False)
    clear_outside((k0,), 0, 9)
    post(r0, k0, g0, c0, 4, 9, 9)

    outs = []

    def write(slot, hbm):
        for t in range(8):
            copy = pltpu.make_async_copy(raw.at[slot, t], hbm.at[:, pl.ds(128 * t, 128)], out_sem.at[slot, t])
            copy.start()
            outs.append(copy)

    for k in range(8):
        unpair(r0, k0, BASE[0] + 8 * k, raw.at[0], 16 * k, 8)
    write(0, sol_hbm)
    residual_pass(s0, r0, k0, g0.at[0], c0, 0, BASE[0], 8, 9, out_tiles=8)
    residual_pass(g0.at[0], k0, r0, g0.at[1], c0, 1, BASE[0], 8, 9, out_tiles=8)
    for k in range(8):
        unpair(s0, g0.at[0], BASE[0] + 8 * k, raw.at[1], 16 * k, 8)
    write(1, res_hbm)
    for copy in outs:
        copy.wait()


def local(right_side, guess):
    def vm(*shape):
        return pltpu.VMEM(shape, F32)

    levels = [vm(2, 8, 128, 128), vm(3, 9, ROWS[0], 128), vm(9, ROWS[0], 128), vm(9, ROWS[0], 128)]
    for l in (1, 2):
        n = OWN[l][1] + 1
        levels += [vm(2, n, ROWS[l], 128)] + [vm(n, ROWS[l], 128)] * 3
    levels += [vm(3, 2, ROWS[3], 128), vm(2, ROWS[3], 128), vm(2, ROWS[3], 128)]
    for l, (pairs, tiles) in enumerate(WHOLE):
        levels += [vm(2, tiles, pairs + 2 * WB, 128)] + [vm(tiles, pairs + 2 * WB, 128)] * (2 if l == 3 else 3)
    coefficients = [vm(10, r, 128) for r in ROWS] + [vm(10, pairs + 2 * WB, 128) for pairs, _ in WHOLE]
    buffers = [
        vm(2, 3, 8, 128), vm(2, 3, 8, 128), vm(4, 3, 8, 128),
        vm(2, 2, 32, 128), vm(4, 2, 24, 128),
        vm(8, 3, 8, 128), vm(8, 128), vm(NA - 1, 8, 128), vm(2, 4, 8, 128),
    ]
    dma = pltpu.SemaphoreType.DMA
    sems = [dma((2, 8)), dma((2, 8))] + [dma((8,))] * 6 + [dma((NA - 1,))] * 2 + [dma((NB - 1,))] * 2
    natural = [vm(1, 48, 128), vm(5, 96, 128), vm(9, 96, 128), vm(4, 64, 128)]
    block = jax.ShapeDtypeStruct(right_side.shape, F32)
    return pl.pallas_call(
        kernel,
        out_shape=(block, block),
        in_specs=[pl.BlockSpec(memory_space=pl.ANY)] * 2,
        out_specs=(pl.BlockSpec(memory_space=pl.ANY),) * 2,
        scratch_shapes=levels + natural + coefficients + buffers + sems,
        compiler_params=pltpu.CompilerParams(collective_id=0, has_side_effects=True),
    )(right_side, guess)


def solution(mesh):
    placed = (P("rad", "ang"), P("rad", "ang"))
    return jax.shard_map(local, mesh=mesh, in_specs=placed, out_specs=placed, check_vma=False)
```

time: 50.6 us -> 46 us (0.909)
  Pallas kernels: 47.1 us -> 42.4 us
    pallas_call x1, Pallas kernels: 47.1 us -> 42.4 us  [local(): pl.pallas_call(kernel, out_shape=(block, block), in_specs=[pl.BlockSpec(m...]
where the time goes in v2:
time: 46 us; the launch traced here: 45.8 us
  Pallas kernels  42.4 us (92%)
  local copies, waits for them, and re-layouts  2.74 us (6%)
  between operations  0.65 us (1%)
    pallas_call x1, Pallas kernels, local(): pl.pallas_call(kernel, out_shape=(block, block), in_specs=[pl.BlockSpec(m...  42.4 us
    unnamed x4, local copies, waits for them, and re-layouts  2.74 us

profile of v2, /device:TPU:1, one launch (start us, length us, event | category | flops | bytes accessed | tf_op | source)
XLA Modules:
  0.0 45.8 jit_solution(315246849872824582)
XLA Ops:
  0.6 42.4 %shard_map.41 = (f32[128,1024]{1,0:T(8,128)}, f32[128,1024]{1,0:T(8,128)}) custom-call(f32[128,1024]{1,0:T(8,128)} %right_hbm.1, f32[128,1024]{1,0:T(8,128)} %guess_hbm.1), custom_call_target="tpu_custom_call" | custom-call | tf_op jit(solution)/shard_map/pallas_call | solution.py:506
  43.1 0.0 copy-start
  43.1 1.9 %copy.6 = f32[128,1024]{1,0:T(8,128)} copy(f32[128,1024]{1,0:T(8,128)} %get-tuple-element.4) | data formatting | bytes 1048576
  45.0 0.0 copy-done
  45.0 0.8 %copy.7 = f32[128,1024]{1,0:T(8,128)} copy(f32[128,1024]{1,0:T(8,128)S(1)} %copy-done) | data formatting | bytes 1048576
Async XLA Ops:
  43.1 2.0 %copy-start = (f32[128,1024]{1,0:T(8,128)S(1)}, f32[128,1024]{1,0:T(8,128)}, u32[]{:S(2)}) copy-start(f32[128,1024]{1,0:T(8,128)} %get-tuple-element.5) | copy-start | bytes 1572868

commit v3 on v2

--- a/solution.py
+++ b/solution.py
@@ -99,28 +99,41 @@
             dst[t, pl.ds(p, 8), :] = c * (new[t] - old[t, pl.ds(p, 8), :])
 
 
-def restricted_block(s, p, n, pairs, lane):
-    even = lane % 2 == 0
-    perm = jnp.where(lane < 64, 2 * lane, 2 * lane - 127)
+def fence(step):
+    pl.when(lax.axis_index("rad") < NB)(step)
+
+
+def joined_block(s, p, n, pairs, lane):
+    even = lane % 2 == 0
     r = [
         3.0 * s[t, pl.ds(p, 8), :] + jnp.where(even, s[t, pl.ds(p + 1, 8), :], s[t, pl.ds(p - 1, 8), :])
         for t in range(n)
     ]
     left, right = ring_shift(r, lane)
     m = [3.0 * r[t] + jnp.where(even, left[t], right[t]) for t in range(n)]
-    out = []
-    for a, b in pairs:
-        joined = jnp.where(even, m[a] + pltpu.roll(m[a], 127, 1), m[b] + pltpu.roll(m[b], 1, 1))
-        out.append(pick(joined, perm) * 0.0625)
-    return out
+    return [
+        jnp.where(even, m[a] + pltpu.roll(m[a], 127, 1), m[b] + pltpu.roll(m[b], 1, 1))
+        for a, b in pairs
+    ]
+
+
+def gathered(x, lane):
+    return pick(x, jnp.where(lane < 64, 2 * lane, 2 * lane - 127)) * 0.0625
 
 
 def restrict_pass(s, fine_base, n, nat, g, coarse_base, c_ref, start, count, pairs):
     _, lane = grid_ids()
     even = lane % 2 == 0
     for k in range(2 * count):
-        for t, x in enumerate(restricted_block(s, fine_base + 2 * start + 8 * k, n, pairs, lane)):
+        for t, x in enumerate(joined_block(s, fine_base + 2 * start + 8 * k, n, pairs, lane)):
             nat[t, pl.ds(8 * k, 8), :] = x
+
+    def gathers():
+        for k in range(2 * count):
+            for t in range(len(pairs)):
+                nat[t, pl.ds(8 * k, 8), :] = gathered(nat[t, pl.ds(8 * k, 8), :], lane)
+
+    fence(gathers)
     for k in range(count):
         p = pl.ds(coarse_base + start + 8 * k, 8)
         red, black = c_ref[3, p, :], c_ref[8, p, :]
@@ -140,20 +153,33 @@
         dst[t, pl.ds(q + 1, 8, stride=2), :] = jnp.where(even, y, x)
 
 
-def prolong_pass(e, f, start, count, fine, fine_base, fine_start, fine_count, plan, sealed):
+def prolong_pass(e, f, fb, start, count, fine, fine_base, fine_start, fine_count, plan, sealed):
     _, lane = grid_ids()
     even = lane % 2 == 0
     half = lane // 2
-    kinds = (half, half + 64, jnp.where(lane < 64, half, half + 64))
     nc = max(source for source, _ in plan) + 1
+
+    def arranged(x, kind):
+        if kind == 0:
+            return x
+        turned = pltpu.roll(x, 64, 1)
+        return turned if kind == 1 else jnp.where(lane < 32, x, turned)
+
     for k in range(count):
         p = FB + start + 8 * k
         x = [e[t, pl.ds(p, 8), :] for t in range(nc)]
         left, right = ring_shift(x, lane)
-        a = [0.75 * x[t] + 0.25 * left[t] for t in range(nc)]
-        b = [0.75 * x[t] + 0.25 * right[t] for t in range(nc)]
         for t, (source, kind) in enumerate(plan):
-            f[t, pl.ds(p, 8), :] = jnp.where(even, pick(a[source], kinds[kind]), pick(b[source], kinds[kind]))
+            f[t, pl.ds(p, 8), :] = arranged(0.75 * x[source] + 0.25 * left[source], kind)
+            fb[t, pl.ds(p, 8), :] = arranged(0.75 * x[source] + 0.25 * right[source], kind)
+
+    def gathers():
+        for k in range(count):
+            at = pl.ds(FB + start + 8 * k, 8)
+            for t in range(len(plan)):
+                f[t, at, :] = jnp.where(even, pick(f[t, at, :], half), pick(fb[t, at, :], half))
+
+    fence(gathers)
     if sealed:
         for t in range(len(plan)):
             f[t, pl.ds(FB - 8, 8), :] = jnp.zeros((8, 128), F32)
@@ -186,17 +212,22 @@
 
 
 def kernel(
-    right_hbm, guess_hbm, sol_hbm, res_hbm,
-    raw, x0, r0, s0, g1, r1, k1, s1, g2, r2, k2, s2, x3, r3, s3,
+    right_hbm, guess_hbm, x0, c0,
+    raw, r0, s0, g1, r1, k1, s1, g2, r2, k2, s2, x3, r3, s3,
     g4, r4, k4, s4, g5, r5, k5, s5, g6, r6, k6, s6, g7, r7, k7,
-    win, e_ref, f_ref, nat, c0, c1, c2, c3, c4, c5, c6, c7,
+    win, e_ref, f_ref, fb_ref, nat, c1, c2, c3, c4, c5, c6, c7,
     pk0, rp0, rd0, rl1, rd1, bs3, own4, slots, strip,
-    load_sem, out_sem, send0, recv0, send1, recv1, sendc, recvc, senda, recva, sendg, recvg,
+    load_sem, send0, recv0, send1, recv1, sendc, recvc, senda, recva, sendg, recvg,
 ):
     me_a, me_r = lax.axis_index("ang"), lax.axis_index("rad")
 
     def device(dr, da):
         return {"ang": lax.rem(me_a + da + NA, NA), "rad": lax.rem(me_r + dr + NB, NB)}
+
+    barrier = pltpu.get_barrier_semaphore()
+    partners = list(DIRS) + [(0, d) for d in range(2, NA - 1)] + [(d, 0) for d in range(2, NB - 1)]
+    for dr, da in partners:
+        pl.semaphore_signal(barrier, inc=1, device_id=device(dr, da), device_id_type=MESH)
 
     loads = []
     for t in range(8):
@@ -205,11 +236,6 @@
                 src.at[:, pl.ds(128 * t, 128)], raw.at[k, t], load_sem.at[k, t]))
     for copy in loads:
         copy.start()
-
-    barrier = pltpu.get_barrier_semaphore()
-    partners = list(DIRS) + [(0, d) for d in range(2, NA - 1)] + [(d, 0) for d in range(2, NB - 1)]
-    for dr, da in partners:
-        pl.semaphore_signal(barrier, inc=1, device_id=device(dr, da), device_id_type=MESH)
 
     zero = jnp.zeros((8, 128), F32)
     k0, g0 = x0.at[0], x0.at[pl.ds(1, 2)]
@@ -359,7 +385,7 @@
     restrict_pass(s2, BASE[2], 3, nat, g3, BASE[3], c3, -4, 2, ((0, 1), (2, 2)))
     down(r3, k3, g3, s3, c3, BASE[3] - 4, 2, 2)
 
-    nat[0, pl.ds(0, 8), :] = restricted_block(s3, BASE[3], 2, ((0, 0),), lane)[0]
+    nat[0, pl.ds(0, 8), :] = gathered(joined_block(s3, BASE[3], 2, ((0, 0),), lane)[0], lane)
     x, y = nat[0, pl.ds(0, 4, stride=2), :], nat[0, pl.ds(1, 4, stride=2), :]
     my_pairs = pl.ds(WB + 4 * me_r, 4)
     own4[pl.ds(0, 4), :] = jnp.where(even[:4], x, y) * c4[3, my_pairs, :]
@@ -407,7 +433,7 @@
     def whole_up(rc, kc, blocks, nc, fine, plan):
         for k in range(blocks):
             unpair(rc, kc, WB + 8 * k, e_ref, FB + 16 * k, nc)
-        prolong_pass(e_ref, f_ref, 0, 2 * blocks, fine, WB, 0, 2 * blocks, plan, True)
+        prolong_pass(e_ref, f_ref, fb_ref, 0, 2 * blocks, fine, WB, 0, 2 * blocks, plan, True)
 
     whole_up(r7, k7, 1, 1, k6, ((0, 0),))
     post(r6, k6, g6, c6, WB, 2, 1)
@@ -439,45 +465,54 @@
         x3[q, 0, pl.ds(BASE[3] + 8, 8), :] = got(1, 0)
         for dr in (-1, 0, 1):
             x3[q, 1, pl.ds(BASE[3] + 8 * dr, 8), :] = jnp.where(lane < 64, got(dr, 1), got(dr, -1))
-    prolong_pass(win, f_ref, -8, 3, k3, BASE[3], -8, 3, ((0, 0), (0, 1)), False)
+    prolong_pass(win, f_ref, fb_ref, -8, 3, k3, BASE[3], -8, 3, ((0, 0), (0, 1)), False)
     clear_outside((k3, g3.at[0], g3.at[1]), 3, 2)
     post(r3, k3, g3, c3, BASE[3] - 8, 3, 2)
 
     for k in range(2):
         unpair(r3, k3, BASE[3] - 4 + 8 * k, e_ref, FB - 8 + 16 * k, 2)
-    prolong_pass(e_ref, f_ref, -8, 4, k2, BASE[2], -4, 3, ((0, 0), (0, 1), (1, 2)), False)
+    prolong_pass(e_ref, f_ref, fb_ref, -8, 4, k2, BASE[2], -4, 3, ((0, 0), (0, 1), (1, 2)), False)
     clear_outside((k2,), 2, 3)
     post(r2, k2, g2, c2, BASE[2] - 4, 3, 3)
 
     for k in range(3):
         unpair(r2, k2, BASE[2] - 4 + 8 * k, e_ref, FB - 8 + 16 * k, 3)
-    prolong_pass(e_ref, f_ref, -8, 6, k1, BASE[1], -4, 5, ((0, 0), (0, 1), (1, 0), (1, 1), (2, 2)), False)
+    prolong_pass(e_ref, f_ref, fb_ref, -8, 6, k1, BASE[1], -4, 5, ((0, 0), (0, 1), (1, 0), (1, 1), (2, 2)), False)
     clear_outside((k1,), 1, 5)
     post(r1, k1, g1, c1, BASE[1] - 4, 5, 5)
 
     for k in range(5):
         unpair(r1, k1, BASE[1] - 4 + 8 * k, e_ref, FB - 8 + 16 * k, 5)
     plan = tuple((t // 2, t % 2) for t in range(8)) + ((4, 2),)
-    prolong_pass(e_ref, f_ref, -8, 10, k0, BASE[0], -4, 9, plan, False)
+    prolong_pass(e_ref, f_ref, fb_ref, -8, 10, k0, BASE[0], -4, 9, plan, False)
     clear_outside((k0,), 0, 9)
-    post(r0, k0, g0, c0, 4, 9, 9)
-
+
+
+def finish(x0, c0, sol_hbm, res_hbm, r, k, s, b, raw, out_sem):
+    zero = jnp.zeros((8, 128), F32)
+    for ref in (r, k):
+        for t in range(9):
+            ref[t, pl.ds(0, 8), :] = zero
+            ref[t, pl.ds(ROWS[0] - 8, 8), :] = zero
+    start, gr, gk = x0.at[0], x0.at[1], x0.at[2]
+    half_sweep(r, start, gr, c0, 0, 4, 9, 9)
+    half_sweep(k, r, gk, c0, 1, 4, 9, 9)
+    half_sweep(r, k, gr, c0, 0, 4, 9, 9)
+    half_sweep(k, r, gk, c0, 1, 4, 9, 9)
     outs = []
 
-    def write(slot, hbm):
+    def write(slot, red, black, hbm):
         for t in range(8):
+            for q in range(8):
+                unpair(red.at[pl.ds(t, 1)], black.at[pl.ds(t, 1)], BASE[0] + 8 * q, raw.at[slot, pl.ds(t, 1)], 16 * q, 1)
             copy = pltpu.make_async_copy(raw.at[slot, t], hbm.at[:, pl.ds(128 * t, 128)], out_sem.at[slot, t])
             copy.start()
             outs.append(copy)
 
-    for k in range(8):
-        unpair(r0, k0, BASE[0] + 8 * k, raw.at[0], 16 * k, 8)
-    write(0, sol_hbm)
-    residual_pass(s0, r0, k0, g0.at[0], c0, 0, BASE[0], 8, 9, out_tiles=8)
-    residual_pass(g0.at[0], k0, r0, g0.at[1], c0, 1, BASE[0], 8, 9, out_tiles=8)
-    for k in range(8):
-        unpair(s0, g0.at[0], BASE[0] + 8 * k, raw.at[1], 16 * k, 8)
-    write(1, res_hbm)
+    write(0, r, k, sol_hbm)
+    residual_pass(s, r, k, gr, c0, 0, BASE[0], 8, 9, out_tiles=8)
+    residual_pass(b, k, r, gk, c0, 1, BASE[0], 8, 9, out_tiles=8)
+    write(1, s, b, res_hbm)
     for copy in outs:
         copy.wait()
 
@@ -486,31 +521,42 @@
     def vm(*shape):
         return pltpu.VMEM(shape, F32)
 
-    levels = [vm(2, 8, 128, 128), vm(3, 9, ROWS[0], 128), vm(9, ROWS[0], 128), vm(9, ROWS[0], 128)]
+    levels = [vm(2, 8, 128, 128), vm(9, ROWS[0], 128), vm(9, ROWS[0], 128)]
     for l in (1, 2):
         n = OWN[l][1] + 1
         levels += [vm(2, n, ROWS[l], 128)] + [vm(n, ROWS[l], 128)] * 3
     levels += [vm(3, 2, ROWS[3], 128), vm(2, ROWS[3], 128), vm(2, ROWS[3], 128)]
     for l, (pairs, tiles) in enumerate(WHOLE):
         levels += [vm(2, tiles, pairs + 2 * WB, 128)] + [vm(tiles, pairs + 2 * WB, 128)] * (2 if l == 3 else 3)
-    coefficients = [vm(10, r, 128) for r in ROWS] + [vm(10, pairs + 2 * WB, 128) for pairs, _ in WHOLE]
+    coefficients = [vm(10, r, 128) for r in ROWS[1:]] + [vm(10, pairs + 2 * WB, 128) for pairs, _ in WHOLE]
     buffers = [
         vm(2, 3, 8, 128), vm(2, 3, 8, 128), vm(4, 3, 8, 128),
         vm(2, 2, 32, 128), vm(4, 2, 24, 128),
         vm(8, 3, 8, 128), vm(8, 128), vm(NA - 1, 8, 128), vm(2, 4, 8, 128),
     ]
     dma = pltpu.SemaphoreType.DMA
-    sems = [dma((2, 8)), dma((2, 8))] + [dma((8,))] * 6 + [dma((NA - 1,))] * 2 + [dma((NB - 1,))] * 2
-    natural = [vm(1, 48, 128), vm(5, 96, 128), vm(9, 96, 128), vm(4, 64, 128)]
-    block = jax.ShapeDtypeStruct(right_side.shape, F32)
-    return pl.pallas_call(
+    sems = [dma((2, 8))] + [dma((8,))] * 6 + [dma((NA - 1,))] * 2 + [dma((NB - 1,))] * 2
+    natural = [vm(1, 48, 128), vm(5, 96, 128), vm(9, 96, 128), vm(9, 96, 128), vm(4, 64, 128)]
+    held = (vm(3, 9, ROWS[0], 128), vm(10, ROWS[0], 128))
+    inside = pl.BlockSpec(memory_space=pltpu.VMEM)
+    outside = pl.BlockSpec(memory_space=pl.ANY)
+    x0, c0 = pl.pallas_call(
         kernel,
-        out_shape=(block, block),
-        in_specs=[pl.BlockSpec(memory_space=pl.ANY)] * 2,
-        out_specs=(pl.BlockSpec(memory_space=pl.ANY),) * 2,
+        out_shape=held,
+        in_specs=[outside] * 2,
+        out_specs=(inside,) * 2,
         scratch_shapes=levels + natural + coefficients + buffers + sems,
         compiler_params=pltpu.CompilerParams(collective_id=0, has_side_effects=True),
     )(right_side, guess)
+    x0, c0 = (pltpu.with_memory_space_constraint(x, pltpu.VMEM) for x in (x0, c0))
+    block = jax.ShapeDtypeStruct(right_side.shape, F32)
+    return pl.pallas_call(
+        finish,
+        out_shape=(block, block),
+        in_specs=[inside] * 2,
+        out_specs=(outside,) * 2,
+        scratch_shapes=[vm(9, ROWS[0], 128)] * 4 + [vm(2, 8, 128, 128), dma((2, 8))],
+    )(x0, c0)
 
 
 def solution(mesh):

time: 46 us -> 42.8 us (0.930)
  local copies, waits for them, and re-layouts: 2.74 us -> 0 us
    unnamed x4 -> x0, local copies, waits for them, and re-layouts: 2.74 us -> none
    pallas_call x1 -> x2, Pallas kernels: 42.4 us -> 42 us  [the longest x1 39.9 us: local(): pl.pallas_call(kernel, out_shape=held, in_specs=[outside] * 2, out_specs=...]
where the time goes in v3:
time: 42.8 us; the launch traced here: 42.6 us
  Pallas kernels  42 us (98%)
  between operations  0.64 us (1%)
    pallas_call x1, Pallas kernels, local(): pl.pallas_call(kernel, out_shape=held, in_specs=[outside] * 2, out_specs=...  39.9 us
    pallas_call x1, Pallas kernels, local(): pl.pallas_call(finish, out_shape=(block, block), in_specs=[inside] * 2, o...  2.07 us

profile of v3, /device:TPU:1, one launch (start us, length us, event | category | flops | bytes accessed | tf_op | source)
XLA Modules:
  0.0 42.6 jit_solution(17038174343909192165)
XLA Ops:
  0.6 39.9 %shard_map.41 = (f32[3,9,80,128]{3,2,1,0:T(8,128)S(1)}, f32[10,80,128]{2,1,0:T(8,128)S(1)}) custom-call(f32[128,1024]{1,0:T(8,128)} %right_hbm.1, f32[128,1024]{1,0:T(8,128)} %guess_hbm.1), custom_call_target="tpu_custom_call" | custom-call | tf_op jit(solution)/shard_map/pallas_call | solution.py:543
  40.6 2.1 %shard_map.42 = (f32[128,1024]{1,0:T(8,128)}, f32[128,1024]{1,0:T(8,128)}) custom-call(f32[3,9,80,128]{3,2,1,0:T(8,128)S(1)} %get-tuple-element.4.x0, f32[10,80,128]{2,1,0:T(8,128)S(1)} %get-tuple-element.5.c0), custom_call_target="tpu_custom_call" | custom-call | tf_op jit(solution)/shard_map/pallas_call | solution.py:553

commit v4 on v3

--- a/solution.py
+++ b/solution.py
@@ -19,6 +19,7 @@
 WB = 8
 DIRS = tuple((dr, da) for dr in (-1, 0, 1) for da in (-1, 0, 1) if dr or da)
 CORNERS = tuple(d for d in DIRS if d[0] and d[1])
+ORDER = tuple(sorted(DIRS, key=lambda d: (d[1] != 0, d[0] == 0)))
 FB = 16
 
 
@@ -192,6 +193,11 @@
             fine[t, at, :] = fine[t, at, :] + (0.75 * f[t, pl.ds(FB + i, 8), :] + 0.25 * other)
 
 
+def wait_bytes(ref, *sems):
+    for sem in sems:
+        pltpu.make_async_copy(ref, ref, sem).wait()
+
+
 def zero_rows(ref, n, start, count):
     for t in range(n):
         for k in range(count):
@@ -211,12 +217,52 @@
         half_sweep(k, r, g.at[1], c, 1, start, count, n)
 
 
+def spread(blocks, reach):
+    return {d: [pltpu.roll(x, -d % 128, 1) if d else x for x in blocks] for d in range(-reach, reach + 1)}
+
+
+def weights(c_ref, count):
+    return [
+        [tuple(c_ref[5 * colour + k, pl.ds(WB + 8 * b, 8), :] for k in range(3)) for b in range(count)]
+        for colour in range(2)
+    ]
+
+
+def relaxed_spread(src, g, w, colour, reach):
+    sub, lane = grid_ids()
+    even = lane % 2 == 0
+    out = {}
+    for d in range(-reach, reach + 1):
+        kind = (colour + d) % 2
+        x = src[d]
+        one = [pltpu.roll(y, 1, 0) for y in x]
+        back = [pltpu.roll(y, 7, 0) for y in x]
+        n = len(x)
+        out[d] = []
+        for b in range(n):
+            before = jnp.where(sub == 0, one[b - 1] if b else 0.0, one[b])
+            after = jnp.where(sub == 7, back[b + 1] if b < n - 1 else 0.0, back[b])
+            near, far, ang = w[kind][b]
+            other = jnp.where(even, before, after) if kind == 0 else jnp.where(even, after, before)
+            out[d].append((g[d][b] + near * x[b]) + (far * other + ang * (src[d - 1][b] + src[d + 1][b])))
+    return out
+
+
+def read(ref, count):
+    return [ref[0, pl.ds(WB + 8 * b, 8), :] for b in range(count)]
+
+
+def put(ref, blocks):
+    for b, x in enumerate(blocks):
+        ref[0, pl.ds(WB + 8 * b, 8), :] = x
+
+
 def kernel(
     right_hbm, guess_hbm, x0, c0,
     raw, r0, s0, g1, r1, k1, s1, g2, r2, k2, s2, x3, r3, s3,
     g4, r4, k4, s4, g5, r5, k5, s5, g6, r6, k6, s6, g7, r7, k7,
     win, e_ref, f_ref, fb_ref, nat, c1, c2, c3, c4, c5, c6, c7,
-    pk0, rp0, rd0, rl1, rd1, bs3, own4, slots, strip,
+    pk0, rp0, rd0, pk1, rl1, rd1, bs3, own4, slots, strip,
     load_sem, send0, recv0, send1, recv1, sendc, recvc, senda, recva, sendg, recvg,
 ):
     me_a, me_r = lax.axis_index("ang"), lax.axis_index("rad")
@@ -233,7 +279,7 @@
     for t in range(8):
         for k, src in ((0, guess_hbm), (1, right_hbm)):
             loads.append(pltpu.make_async_copy(
-                src.at[:, pl.ds(128 * t, 128)], raw.at[k, t], load_sem.at[k, t]))
+                src.at[:, pl.ds(128 * t, 128)], raw.at[k, t], load_sem))
     for copy in loads:
         copy.start()
 
@@ -267,18 +313,17 @@
     sub, lane = grid_ids()
     even = lane % 2 == 0
 
-    def remote(src, dst, sems, recvs, k, dr, da):
-        return pltpu.make_async_remote_copy(
-            src_ref=src, dst_ref=dst, send_sem=sems.at[k], recv_sem=recvs.at[k],
-            device_id=device(dr, da), device_id_type=MESH)
+    def send(src, dst, send_sem, recv_sem, dr, da):
+        pltpu.make_async_remote_copy(
+            src_ref=src, dst_ref=dst, send_sem=send_sem, recv_sem=recv_sem,
+            device_id=device(dr, da), device_id_type=MESH).start()
 
     def edge(l, dr, width):
         if dr < 0:
             return pl.ds(BASE[l], width), pl.ds(BASE[l] + OWN[l][0], width)
         return pl.ds(BASE[l] + OWN[l][0] - width, width), pl.ds(BASE[l] - width, width)
 
-    for copy in loads:
-        copy.wait()
+    wait_bytes(raw, load_sem)
     for k in range(8):
         at = pl.ds(BASE[0] + 8 * k, 8)
         red, black = c0[3, at, :], c0[8, at, :]
@@ -300,23 +345,20 @@
             pk0[side, q, :, :] = total
     pl.semaphore_wait(barrier, len(partners))
 
-    sends = []
-    for k, (dr, da) in enumerate(DIRS):
+    for dr, da in ORDER:
+        mine, theirs = edge(0, dr, E0) if dr else (None, None)
         if da == 0:
-            mine, theirs = edge(0, dr, E0)
-            copy = remote(x0.at[:, pl.ds(0, 8), mine, :], x0.at[:, pl.ds(0, 8), theirs, :], send0, recv0, k, dr, da)
+            send(x0.at[0, pl.ds(0, 8), mine, :], x0.at[0, pl.ds(0, 8), theirs, :], send0, recv0, dr, da)
+            mine, theirs = edge(0, dr, 4)
+            send(x0.at[pl.ds(1, 2), pl.ds(0, 8), mine, :], x0.at[pl.ds(1, 2), pl.ds(0, 8), theirs, :],
+                 send0, recv0, dr, da)
         elif dr == 0:
             side = 0 if da < 0 else 1
-            copy = remote(pk0.at[side], rp0.at[side], send0, recv0, k, dr, da)
+            send(pk0.at[side], rp0.at[side], send0, recv0, dr, da)
         else:
-            mine, _ = edge(0, dr, E0)
             tile = 0 if da < 0 else 7
-            copy = remote(
-                x0.at[:, tile, mine, :], rd0.at[CORNERS.index((dr, da)), :, pl.ds(0, E0), :], send0, recv0, k, dr, da)
-        copy.start()
-        sends.append(copy)
-    for copy in sends:
-        copy.wait()
+            send(x0.at[:, tile, mine, :], rd0.at[CORNERS.index((dr, da)), :, pl.ds(0, E0), :], send0, recv0, dr, da)
+    wait_bytes(f_ref.at[pl.ds(0, 4), pl.ds(0, 79), :], send0, recv0)
 
     def clear_outside(refs, l, n, depth=1):
         @pl.when(me_r == 0)
@@ -349,31 +391,37 @@
     residual_pass(s0, r0, k0, g0.at[0], c0, 0, 4, 9, 9)
     restrict_pass(s0, BASE[0], 9, nat, g1, BASE[1], c1, 0, 4, ((0, 1), (2, 3), (4, 5), (6, 7)))
 
-    sends = []
-    for k, (dr, da) in enumerate(DIRS):
-        tile = 0 if da < 0 else 3
-        mine, theirs = edge(1, dr, E1) if dr else (pl.ds(BASE[1], 32), None)
+    for b in range(4):
+        at, own = pl.ds(8 * b, 8), pl.ds(BASE[1] + 8 * b, 8)
+        pk1[0, at, :] = jnp.where(lane < 64, g1[0, 0, own, :], pltpu.roll(g1[1, 0, own, :], 64, 1))
+        pk1[1, at, :] = jnp.where(lane < 64, pltpu.roll(g1[0, 3, own, :], 64, 1), g1[1, 3, own, :])
+    for dr, da in ORDER:
+        side = 0 if da < 0 else 1
         if da == 0:
-            copy = remote(g1.at[:, pl.ds(0, 4), mine, :], g1.at[:, pl.ds(0, 4), theirs, :], send1, recv1, k, dr, da)
+            mine, theirs = edge(1, dr, E1)
+            send(g1.at[:, pl.ds(0, 4), mine, :], g1.at[:, pl.ds(0, 4), theirs, :], send1, recv1, dr, da)
         elif dr == 0:
-            copy = remote(g1.at[:, tile, mine, :], rl1.at[0 if da < 0 else 1], send1, recv1, k, dr, da)
+            send(pk1.at[side], rl1.at[side], send1, recv1, dr, da)
         else:
-            copy = remote(
-                g1.at[:, tile, mine, :], rd1.at[CORNERS.index((dr, da)), :, pl.ds(0, E1), :], send1, recv1, k, dr, da)
-        copy.start()
-        sends.append(copy)
-    for copy in sends:
-        copy.wait()
+            send(pk1.at[side, pl.ds(0 if dr < 0 else 32 - E1, E1), :],
+                 rd1.at[CORNERS.index((dr, da)), pl.ds(0, E1), :], send1, recv1, dr, da)
+    wait_bytes(f_ref.at[pl.ds(0, 8), pl.ds(0, 53), :], send1, recv1)
+
+    def merge_edges(row, size, from_right, from_left):
+        low = lane[:size] < 64
+        g1[0, 4, pl.ds(row, size), :] = jnp.where(low, from_right, pltpu.roll(from_left, 64, 1))
+        g1[1, 4, pl.ds(row, size), :] = jnp.where(low, pltpu.roll(from_right, 64, 1), from_left)
+
+    for b in range(4):
+        merge_edges(BASE[1] + 8 * b, 8, rl1[0, pl.ds(8 * b, 8), :], rl1[1, pl.ds(8 * b, 8), :])
+    for dr in (-1, 1):
+        start = BASE[1] - E1 if dr < 0 else BASE[1] + OWN[1][0]
+        right, left = CORNERS.index((-dr, -1)), CORNERS.index((-dr, 1))
+        for first in (0, 8, 16):
+            size = 8 if first < 16 else 2
+            merge_edges(start + first, size, rd1[right, pl.ds(first, size), :], rd1[left, pl.ds(first, size), :])
     for q in range(2):
-        for b in range(4):
-            g1[q, 4, pl.ds(BASE[1] + 8 * b, 8), :] = jnp.where(
-                lane < 64, rl1[0, q, pl.ds(8 * b, 8), :], rl1[1, q, pl.ds(8 * b, 8), :])
         for dr in (-1, 1):
-            start = BASE[1] - E1 if dr < 0 else BASE[1] + OWN[1][0]
-            for first, size in ((0, 8), (8, 8), (16, 2)):
-                x = rd1[CORNERS.index((-dr, -1)), q, pl.ds(first, size), :]
-                y = rd1[CORNERS.index((-dr, 1)), q, pl.ds(first, size), :]
-                g1[q, 4, pl.ds(start + first, size), :] = jnp.where(lane[:size] < 64, x, y)
             rest = BASE[1] - E1 - 3 if dr < 0 else BASE[1] + OWN[1][0] + E1
             for t in range(5):
                 g1[q, t, pl.ds(rest, 3), :] = jnp.zeros((3, 128), F32)
@@ -390,18 +438,9 @@
     my_pairs = pl.ds(WB + 4 * me_r, 4)
     own4[pl.ds(0, 4), :] = jnp.where(even[:4], x, y) * c4[3, my_pairs, :]
     own4[pl.ds(4, 4), :] = jnp.where(even[:4], y, x) * c4[8, my_pairs, :]
-    ring = []
     for d in range(1, NA):
-        copy = remote(own4, slots.at[d - 1], senda, recva, d - 1, 0, d)
-        copy.start()
-        ring.append(copy)
-    back3 = []
-    for k, (dr, da) in enumerate(DIRS):
-        copy = remote(x3.at[:, 0, pl.ds(BASE[3], 8), :], bs3.at[k], sendc, recvc, k, dr, da)
-        copy.start()
-        back3.append(copy)
-    for copy in ring:
-        copy.wait()
+        send(own4, slots.at[d - 1], senda, recva, 0, d)
+    wait_bytes(slots, senda, recva)
     for t in range(4):
         total = own4[...]
         for d in range(1, NA):
@@ -411,24 +450,34 @@
         for q in range(2):
             strip[q, t, pl.ds(0, 4), :] = total[4 * q:4 * q + 4]
             g4[q, t, my_pairs, :] = total[4 * q:4 * q + 4]
-    column = []
     for d in range(1, NB):
-        copy = remote(strip.at[:, :, pl.ds(0, 4), :], g4.at[:, :, my_pairs, :], sendg, recvg, d - 1, d, 0)
-        copy.start()
-        column.append(copy)
-    for copy in column:
-        copy.wait()
+        send(strip.at[:, :, pl.ds(0, 4), :], g4.at[:, :, my_pairs, :], sendg, recvg, d, 0)
+    for k, (dr, da) in enumerate(DIRS):
+        send(x3.at[:, 0, pl.ds(BASE[3], 8), :], bs3.at[k], sendc, recvc, dr, da)
+    wait_bytes(g4.at[:, :, pl.ds(WB, 60), :], sendg, recvg)
 
     down(r4, k4, g4, s4, c4, WB, 8, 4)
     restrict_pass(s4, WB, 4, nat, g5, WB, c5, 0, 4, ((0, 1), (2, 3)))
     down(r5, k5, g5, s5, c5, WB, 4, 2)
     restrict_pass(s5, WB, 2, nat, g6, WB, c6, 0, 2, ((0, 1),))
-    down(r6, k6, g6, s6, c6, WB, 2, 1)
+    gr6, gk6, w6 = spread(read(g6.at[0], 2), 4), spread(read(g6.at[1], 2), 3), weights(c6, 2)
+    black = relaxed_spread(gr6, gk6, w6, 1, 3)
+    red = relaxed_spread(black, gr6, w6, 0, 2)
+    black = relaxed_spread(red, gk6, w6, 1, 1)
+    put(k6, black[0])
+    new = relaxed_spread(black, gr6, w6, 0, 0)[0]
+    put(s6, [c6[4, pl.ds(WB + 8 * b, 8), :] * (new[b] - red[0][b]) for b in range(2)])
     restrict_pass(s6, WB, 1, nat, g7, WB, c7, 0, 1, ((0, 0),))
-    half_sweep(k7, g7.at[0], g7.at[1], c7, 1, WB, 1, 1)
-    for _ in range(7):
-        half_sweep(r7, k7, g7.at[0], c7, 0, WB, 1, 1)
-        half_sweep(k7, r7, g7.at[1], c7, 1, WB, 1, 1)
+    gr7, gk7, w7 = spread(read(g7.at[0], 1), 4), spread(read(g7.at[1], 1), 3), weights(c7, 1)
+    source = gr7
+    for step in range(4):
+        black = relaxed_spread(source, gk7, w7, 1, 3 if step < 3 else 2)
+        red = relaxed_spread(black, gr7, w7, 0, 2 if step < 3 else 1)
+        black = relaxed_spread(red, gk7, w7, 1, 1 if step < 3 else 0)
+        if step < 3:
+            source = spread(relaxed_spread(black, gr7, w7, 0, 0)[0], 4)
+    put(r7, red[0])
+    put(k7, black[0])
 
     def whole_up(rc, kc, blocks, nc, fine, plan):
         for k in range(blocks):
@@ -436,7 +485,11 @@
         prolong_pass(e_ref, f_ref, fb_ref, 0, 2 * blocks, fine, WB, 0, 2 * blocks, plan, True)
 
     whole_up(r7, k7, 1, 1, k6, ((0, 0),))
-    post(r6, k6, g6, c6, WB, 2, 1)
+    red = relaxed_spread(spread(read(k6, 2), 4), gr6, w6, 0, 3)
+    black = relaxed_spread(red, gk6, w6, 1, 2)
+    red = relaxed_spread(black, gr6, w6, 0, 1)
+    put(r6, red[0])
+    put(k6, relaxed_spread(red, gk6, w6, 1, 0)[0])
     whole_up(r6, k6, 2, 1, k5, ((0, 0), (0, 1)))
     post(r5, k5, g5, c5, WB, 4, 2)
     whole_up(r5, k5, 4, 2, k4, ((0, 0), (0, 1), (1, 0), (1, 1)))
@@ -457,8 +510,7 @@
         win[0, pl.ds(q, 8, stride=2), :] = jnp.where(even, seen[0], seen[1])
         win[0, pl.ds(q + 1, 8, stride=2), :] = jnp.where(even, seen[1], seen[0])
 
-    for copy in back3:
-        copy.wait()
+    wait_bytes(bs3, sendc, recvc)
     for q in range(3):
         got = lambda dr, da: bs3[DIRS.index((-dr, -da)), q]
         x3[q, 0, pl.ds(BASE[3] - 8, 8), :] = got(-1, 0)
@@ -499,22 +551,19 @@
     half_sweep(k, r, gk, c0, 1, 4, 9, 9)
     half_sweep(r, k, gr, c0, 0, 4, 9, 9)
     half_sweep(k, r, gk, c0, 1, 4, 9, 9)
-    outs = []
 
     def write(slot, red, black, hbm):
         for t in range(8):
             for q in range(8):
                 unpair(red.at[pl.ds(t, 1)], black.at[pl.ds(t, 1)], BASE[0] + 8 * q, raw.at[slot, pl.ds(t, 1)], 16 * q, 1)
-            copy = pltpu.make_async_copy(raw.at[slot, t], hbm.at[:, pl.ds(128 * t, 128)], out_sem.at[slot, t])
+            copy = pltpu.make_async_copy(raw.at[slot, t], hbm.at[:, pl.ds(128 * t, 128)], out_sem)
             copy.start()
-            outs.append(copy)
 
     write(0, r, k, sol_hbm)
     residual_pass(s, r, k, gr, c0, 0, BASE[0], 8, 9, out_tiles=8)
     residual_pass(b, k, r, gk, c0, 1, BASE[0], 8, 9, out_tiles=8)
     write(1, s, b, res_hbm)
-    for copy in outs:
-        copy.wait()
+    wait_bytes(raw, out_sem)
 
 
 def local(right_side, guess):
@@ -531,11 +580,11 @@
     coefficients = [vm(10, r, 128) for r in ROWS[1:]] + [vm(10, pairs + 2 * WB, 128) for pairs, _ in WHOLE]
     buffers = [
         vm(2, 3, 8, 128), vm(2, 3, 8, 128), vm(4, 3, 8, 128),
-        vm(2, 2, 32, 128), vm(4, 2, 24, 128),
+        vm(2, 32, 128), vm(2, 32, 128), vm(4, 24, 128),
         vm(8, 3, 8, 128), vm(8, 128), vm(NA - 1, 8, 128), vm(2, 4, 8, 128),
     ]
     dma = pltpu.SemaphoreType.DMA
-    sems = [dma((2, 8))] + [dma((8,))] * 6 + [dma((NA - 1,))] * 2 + [dma((NB - 1,))] * 2
+    sems = [dma] * 11
     natural = [vm(1, 48, 128), vm(5, 96, 128), vm(9, 96, 128), vm(9, 96, 128), vm(4, 64, 128)]
     held = (vm(3, 9, ROWS[0], 128), vm(10, ROWS[0], 128))
     inside = pl.BlockSpec(memory_space=pltpu.VMEM)
@@ -555,7 +604,7 @@
         out_shape=(block, block),
         in_specs=[inside] * 2,
         out_specs=(outside,) * 2,
-        scratch_shapes=[vm(9, ROWS[0], 128)] * 4 + [vm(2, 8, 128, 128), dma((2, 8))],
+        scratch_shapes=[vm(9, ROWS[0], 128)] * 4 + [vm(2, 8, 128, 128), dma],
     )(x0, c0)
 
 

time: 42.8 us -> 40.8 us (0.953)
  Pallas kernels: 42 us -> 40 us
    pallas_call x1, Pallas kernels: 39.9 us -> 38.1 us  [local(): pl.pallas_call(kernel, out_shape=held, in_specs=[outside] * 2, out_specs=...]
where the time goes in v4:
time: 40.8 us; the launch traced here: 40.7 us
  Pallas kernels  40 us (98%)
  between operations  0.64 us (2%)
    pallas_call x1, Pallas kernels, local(): pl.pallas_call(kernel, out_shape=held, in_specs=[outside] * 2, out_specs=...  38.1 us
    pallas_call x1, Pallas kernels, local(): pl.pallas_call(finish, out_shape=(block, block), in_specs=[inside] * 2, o...  1.94 us

profile of v4, /device:TPU:1, one launch (start us, length us, event | category | flops | bytes accessed | tf_op | source)
XLA Modules:
  0.0 40.7 jit_solution(12895422219939381701)
XLA Ops:
  0.6 38.1 %shard_map.41 = (f32[3,9,80,128]{3,2,1,0:T(8,128)S(1)}, f32[10,80,128]{2,1,0:T(8,128)S(1)}) custom-call(f32[128,1024]{1,0:T(8,128)} %right_hbm.1, f32[128,1024]{1,0:T(8,128)} %guess_hbm.1), custom_call_target="tpu_custom_call" | custom-call | tf_op jit(solution)/shard_map/pallas_call | solution.py:592
  38.7 1.9 %shard_map.42 = (f32[128,1024]{1,0:T(8,128)}, f32[128,1024]{1,0:T(8,128)}) custom-call(f32[3,9,80,128]{3,2,1,0:T(8,128)S(1)} %get-tuple-element.4.x0, f32[10,80,128]{2,1,0:T(8,128)S(1)} %get-tuple-element.5.c0), custom_call_target="tpu_custom_call" | custom-call | tf_op jit(solution)/shard_map/pallas_call | solution.py:602

commit v5 on v4

--- a/solution.py
+++ b/solution.py
@@ -67,67 +67,78 @@
             c_ref[5 + j, at, :] = jnp.where(even, y, x)
 
 
-def relaxed(src, g, c_ref, colour, p, n, lane):
+def relaxed(src, g, c_ref, colour, p, n, lane, tiles):
     at = pl.ds(p, 8)
     even = lane % 2 == 0
     first, second = (p - 1, p + 1) if colour == 0 else (p + 1, p - 1)
-    x = [src[t, at, :] for t in range(n)]
-    left, right = ring_shift(x, lane)
+    x = {t: src[t, at, :] for t in sorted({(u + d) % n for u in tiles for d in (-1, 0, 1)})}
+    one = {t: pltpu.roll(x[t], 1, 1) for t in sorted({(u + d) % n for u in tiles for d in (-1, 0)})}
+    back = {t: pltpu.roll(x[t], 127, 1) for t in sorted({(u + d) % n for u in tiles for d in (0, 1)})}
     near, far, ang = (c_ref[5 * colour + k, at, :] for k in range(3))
-    return [
-        (g[t, at, :] + near * x[t])
-        + (far * jnp.where(even, src[t, pl.ds(first, 8), :], src[t, pl.ds(second, 8), :]) + ang * (left[t] + right[t]))
-        for t in range(n)
-    ]
-
-
-def half_sweep(dst, src, g, c_ref, colour, start, count, n):
+    new = {}
+    for t in tiles:
+        left, right = one[t], back[t]
+        if n > 1:
+            left = jnp.where(lane == 0, one[(t - 1) % n], left)
+            right = jnp.where(lane == 127, back[(t + 1) % n], right)
+        other = jnp.where(even, src[t, pl.ds(first, 8), :], src[t, pl.ds(second, 8), :])
+        new[t] = (g[t, at, :] + near * x[t]) + (far * other + ang * (left + right))
+    return new
+
+
+def half_sweep(dst, src, g, c_ref, colour, start, count, n, tiles=None):
     _, lane = grid_ids()
     for k in range(count):
         p = start + 8 * k
-        new = relaxed(src, g, c_ref, colour, p, n, lane)
-        for t in range(n):
-            dst[t, pl.ds(p, 8), :] = new[t]
-
-
-def residual_pass(dst, old, src, g, c_ref, colour, start, count, n, out_tiles=None):
+        for t, value in relaxed(src, g, c_ref, colour, p, n, lane, tiles or range(n)).items():
+            dst[t, pl.ds(p, 8), :] = value
+
+
+def residual_pass(dst, old, src, g, c_ref, colour, start, count, n, tiles=None):
     _, lane = grid_ids()
     for k in range(count):
         p = start + 8 * k
-        new = relaxed(src, g, c_ref, colour, p, n, lane)
         c = c_ref[5 * colour + 4, pl.ds(p, 8), :]
-        for t in range(out_tiles or n):
-            dst[t, pl.ds(p, 8), :] = c * (new[t] - old[t, pl.ds(p, 8), :])
+        for t, value in relaxed(src, g, c_ref, colour, p, n, lane, tiles or range(n)).items():
+            dst[t, pl.ds(p, 8), :] = c * (value - old[t, pl.ds(p, 8), :])
 
 
 def fence(step):
     pl.when(lax.axis_index("rad") < NB)(step)
 
 
-def joined_block(s, p, n, pairs, lane):
+def mixed_block(s, p, n, lane):
     even = lane % 2 == 0
     r = [
         3.0 * s[t, pl.ds(p, 8), :] + jnp.where(even, s[t, pl.ds(p + 1, 8), :], s[t, pl.ds(p - 1, 8), :])
         for t in range(n)
     ]
     left, right = ring_shift(r, lane)
-    m = [3.0 * r[t] + jnp.where(even, left[t], right[t]) for t in range(n)]
-    return [
-        jnp.where(even, m[a] + pltpu.roll(m[a], 127, 1), m[b] + pltpu.roll(m[b], 1, 1))
-        for a, b in pairs
-    ]
+    return [3.0 * r[t] + jnp.where(even, left[t], right[t]) for t in range(n)]
+
+
+def joined(a, b, lane):
+    return jnp.where(lane % 2 == 0, a + pltpu.roll(a, 127, 1), b + pltpu.roll(b, 1, 1))
 
 
 def gathered(x, lane):
     return pick(x, jnp.where(lane < 64, 2 * lane, 2 * lane - 127)) * 0.0625
 
 
-def restrict_pass(s, fine_base, n, nat, g, coarse_base, c_ref, start, count, pairs):
+def restrict_pass(s, fine_base, n, mix, nat, g, coarse_base, c_ref, start, count, pairs):
     _, lane = grid_ids()
     even = lane % 2 == 0
     for k in range(2 * count):
-        for t, x in enumerate(joined_block(s, fine_base + 2 * start + 8 * k, n, pairs, lane)):
-            nat[t, pl.ds(8 * k, 8), :] = x
+        for t, x in enumerate(mixed_block(s, fine_base + 2 * start + 8 * k, n, lane)):
+            mix[t, pl.ds(8 * k, 8), :] = x
+
+    def joins():
+        for k in range(2 * count):
+            at = pl.ds(8 * k, 8)
+            for t, (a, b) in enumerate(pairs):
+                nat[t, at, :] = joined(mix[a, at, :], mix[b, at, :], lane)
+
+    fence(joins)
 
     def gathers():
         for k in range(2 * count):
@@ -217,13 +228,25 @@
         half_sweep(k, r, g.at[1], c, 1, start, count, n)
 
 
-def spread(blocks, reach):
-    return {d: [pltpu.roll(x, -d % 128, 1) if d else x for x in blocks] for d in range(-reach, reach + 1)}
-
-
-def weights(c_ref, count):
+def spread(tiles, reach):
+    _, lane = grid_ids()
+    n = len(tiles)
+    out = {0: tiles}
+    for d in [k for k in range(-reach, reach + 1) if k]:
+        turned = [[pltpu.roll(x, -d % 128, 1) for x in blocks] for blocks in tiles]
+        if n > 1:
+            own = lane < 128 - d if d > 0 else lane >= -d
+            step = 1 if d > 0 else -1
+            turned = [
+                [jnp.where(own, x, y) for x, y in zip(turned[t], turned[(t + step) % n])] for t in range(n)
+            ]
+        out[d] = turned
+    return out
+
+
+def weights(c_ref, start, count):
     return [
-        [tuple(c_ref[5 * colour + k, pl.ds(WB + 8 * b, 8), :] for k in range(3)) for b in range(count)]
+        [tuple(c_ref[5 * colour + k, pl.ds(start + 8 * b, 8), :] for k in range(3)) for b in range(count)]
         for colour in range(2)
     ]
 
@@ -234,35 +257,62 @@
     out = {}
     for d in range(-reach, reach + 1):
         kind = (colour + d) % 2
-        x = src[d]
-        one = [pltpu.roll(y, 1, 0) for y in x]
-        back = [pltpu.roll(y, 7, 0) for y in x]
-        n = len(x)
         out[d] = []
-        for b in range(n):
-            before = jnp.where(sub == 0, one[b - 1] if b else 0.0, one[b])
-            after = jnp.where(sub == 7, back[b + 1] if b < n - 1 else 0.0, back[b])
-            near, far, ang = w[kind][b]
-            other = jnp.where(even, before, after) if kind == 0 else jnp.where(even, after, before)
-            out[d].append((g[d][b] + near * x[b]) + (far * other + ang * (src[d - 1][b] + src[d + 1][b])))
+        for t, x in enumerate(src[d]):
+            one = [pltpu.roll(y, 1, 0) for y in x]
+            back = [pltpu.roll(y, 7, 0) for y in x]
+            n = len(x)
+            new = []
+            for b in range(n):
+                before = jnp.where(sub == 0, one[b - 1] if b else 0.0, one[b])
+                after = jnp.where(sub == 7, back[b + 1] if b < n - 1 else 0.0, back[b])
+                near, far, ang = w[kind][b]
+                other = jnp.where(even, before, after) if kind == 0 else jnp.where(even, after, before)
+                new.append((g[d][t][b] + near * x[b]) + (far * other + ang * (src[d - 1][t][b] + src[d + 1][t][b])))
+            out[d].append(new)
     return out
 
 
-def read(ref, count):
-    return [ref[0, pl.ds(WB + 8 * b, 8), :] for b in range(count)]
-
-
-def put(ref, blocks):
-    for b, x in enumerate(blocks):
-        ref[0, pl.ds(WB + 8 * b, 8), :] = x
+def read(ref, start, count, n=1):
+    return [[ref[t, pl.ds(start + 8 * b, 8), :] for b in range(count)] for t in range(n)]
+
+
+def put(ref, start, tiles):
+    for t, blocks in enumerate(tiles):
+        for b, x in enumerate(blocks):
+            ref[t, pl.ds(start + 8 * b, 8), :] = x
+
+
+def spread_down(k, g, s, c_ref, start, count, n):
+    w = weights(c_ref, start, count)
+    gr, gk = spread(read(g.at[0], start, count, n), 4), spread(read(g.at[1], start, count, n), 3)
+    black = relaxed_spread(gr, gk, w, 1, 3)
+    red = relaxed_spread(black, gr, w, 0, 2)
+    black = relaxed_spread(red, gk, w, 1, 1)
+    put(k, start, black[0])
+    new = relaxed_spread(black, gr, w, 0, 0)[0]
+    for t in range(n):
+        for b in range(count):
+            at = pl.ds(start + 8 * b, 8)
+            s[t, at, :] = c_ref[4, at, :] * (new[t][b] - red[0][t][b])
+
+
+def spread_post(r, k, g, c_ref, start, count, n):
+    w = weights(c_ref, start, count)
+    gr, gk = spread(read(g.at[0], start, count, n), 3), spread(read(g.at[1], start, count, n), 2)
+    red = relaxed_spread(spread(read(k, start, count, n), 4), gr, w, 0, 3)
+    black = relaxed_spread(red, gk, w, 1, 2)
+    red = relaxed_spread(black, gr, w, 0, 1)
+    put(r, start, red[0])
+    put(k, start, relaxed_spread(red, gk, w, 1, 0)[0])
 
 
 def kernel(
     right_hbm, guess_hbm, x0, c0,
     raw, r0, s0, g1, r1, k1, s1, g2, r2, k2, s2, x3, r3, s3,
     g4, r4, k4, s4, g5, r5, k5, s5, g6, r6, k6, s6, g7, r7, k7,
-    win, e_ref, f_ref, fb_ref, nat, c1, c2, c3, c4, c5, c6, c7,
-    pk0, rp0, rd0, pk1, rl1, rd1, bs3, own4, slots, strip,
+    win, e_ref, f_ref, fb_ref, mix, nat, c1, c2, c3, c4, c5, c6, c7,
+    pk0, pc0, rp0, rd0, pk1, rl1, rd1, bs3, own4, slots, strip,
     load_sem, send0, recv0, send1, recv1, sendc, recvc, senda, recva, sendg, recvg,
 ):
     me_a, me_r = lax.axis_index("ang"), lax.axis_index("rad")
@@ -343,6 +393,16 @@
                 x = pltpu.roll(x, shift, 1) if shift else x
                 total = x if total is None else jnp.where(lane // 16 == b, x, total)
             pk0[side, q, :, :] = total
+    for c, (dr, da) in enumerate(CORNERS):
+        rows = pl.ds(BASE[0] if dr < 0 else BASE[0] + OWN[0][0] - 8, 8)
+        tile, first = (0, 0) if da < 0 else (7, 112)
+        total = None
+        for q in range(3):
+            x = x0[q, tile, rows, :]
+            shift = (16 * q - first) % 128
+            x = pltpu.roll(x, shift, 1) if shift else x
+            total = x if total is None else jnp.where(lane // 16 == q, x, total)
+        pc0[c, :, :] = total
     pl.semaphore_wait(barrier, len(partners))
 
     for dr, da in ORDER:
@@ -356,9 +416,9 @@
             side = 0 if da < 0 else 1
             send(pk0.at[side], rp0.at[side], send0, recv0, dr, da)
         else:
-            tile = 0 if da < 0 else 7
-            send(x0.at[:, tile, mine, :], rd0.at[CORNERS.index((dr, da)), :, pl.ds(0, E0), :], send0, recv0, dr, da)
-    wait_bytes(f_ref.at[pl.ds(0, 4), pl.ds(0, 79), :], send0, recv0)
+            c = CORNERS.index((dr, da))
+            send(pc0.at[c, pl.ds(0 if dr < 0 else 8 - E0, E0), :], rd0.at[c, pl.ds(0, E0), :], send0, recv0, dr, da)
+    wait_bytes(f_ref.at[pl.ds(0, 4), pl.ds(0, 69), :], send0, recv0)
 
     def clear_outside(refs, l, n, depth=1):
         @pl.when(me_r == 0)
@@ -380,16 +440,17 @@
             x0[q, 8, pl.ds(BASE[0] + 8 * b, 8), :] = jnp.where(lane < 64, x, y)
         for dr in (-1, 1):
             start = BASE[0] - E0 if dr < 0 else BASE[0] + OWN[0][0]
-            x = rd0[CORNERS.index((-dr, -1)), q, pl.ds(0, E0), :]
-            y = rd0[CORNERS.index((-dr, 1)), q, pl.ds(0, E0), :]
-            x0[q, 8, pl.ds(start, E0), :] = jnp.where(lane[:E0] < 64, x, y)
+            x = rd0[CORNERS.index((-dr, -1)), :, :]
+            y = pltpu.roll(rd0[CORNERS.index((-dr, 1)), :, :], 112 - 16 * q, 1)
+            x = pltpu.roll(x, 128 - 16 * q, 1) if q else x
+            x0[q, 8, pl.ds(start, E0), :] = jnp.where(lane < 64, x, y)[:E0]
     clear_outside((k0, g0.at[0], g0.at[1]), 0, 9)
 
     for _ in range(2):
         half_sweep(r0, k0, g0.at[0], c0, 0, 4, 9, 9)
         half_sweep(k0, r0, g0.at[1], c0, 1, 4, 9, 9)
     residual_pass(s0, r0, k0, g0.at[0], c0, 0, 4, 9, 9)
-    restrict_pass(s0, BASE[0], 9, nat, g1, BASE[1], c1, 0, 4, ((0, 1), (2, 3), (4, 5), (6, 7)))
+    restrict_pass(s0, BASE[0], 9, mix, nat, g1, BASE[1], c1, 0, 4, ((0, 1), (2, 3), (4, 5), (6, 7)))
 
     for b in range(4):
         at, own = pl.ds(8 * b, 8), pl.ds(BASE[1] + 8 * b, 8)
@@ -428,12 +489,12 @@
     clear_outside((g1.at[0], g1.at[1]), 1, 5, 3)
 
     down(r1, k1, g1, s1, c1, BASE[1] - 20, 9, 5)
-    restrict_pass(s1, BASE[1], 5, nat, g2, BASE[2], c2, -8, 4, ((0, 1), (2, 3), (4, 4)))
+    restrict_pass(s1, BASE[1], 5, mix, nat, g2, BASE[2], c2, -8, 4, ((0, 1), (2, 3), (4, 4)))
     down(r2, k2, g2, s2, c2, BASE[2] - 8, 4, 3)
-    restrict_pass(s2, BASE[2], 3, nat, g3, BASE[3], c3, -4, 2, ((0, 1), (2, 2)))
-    down(r3, k3, g3, s3, c3, BASE[3] - 4, 2, 2)
-
-    nat[0, pl.ds(0, 8), :] = gathered(joined_block(s3, BASE[3], 2, ((0, 0),), lane)[0], lane)
+    restrict_pass(s2, BASE[2], 3, mix, nat, g3, BASE[3], c3, -4, 2, ((0, 1), (2, 2)))
+    spread_down(k3, g3, s3, c3, BASE[3] - 4, 2, 2)
+
+    nat[0, pl.ds(0, 8), :] = gathered(joined(*mixed_block(s3, BASE[3], 2, lane)[:1] * 2, lane), lane)
     x, y = nat[0, pl.ds(0, 4, stride=2), :], nat[0, pl.ds(1, 4, stride=2), :]
     my_pairs = pl.ds(WB + 4 * me_r, 4)
     own4[pl.ds(0, 4), :] = jnp.where(even[:4], x, y) * c4[3, my_pairs, :]
@@ -457,18 +518,12 @@
     wait_bytes(g4.at[:, :, pl.ds(WB, 60), :], sendg, recvg)
 
     down(r4, k4, g4, s4, c4, WB, 8, 4)
-    restrict_pass(s4, WB, 4, nat, g5, WB, c5, 0, 4, ((0, 1), (2, 3)))
+    restrict_pass(s4, WB, 4, mix, nat, g5, WB, c5, 0, 4, ((0, 1), (2, 3)))
     down(r5, k5, g5, s5, c5, WB, 4, 2)
-    restrict_pass(s5, WB, 2, nat, g6, WB, c6, 0, 2, ((0, 1),))
-    gr6, gk6, w6 = spread(read(g6.at[0], 2), 4), spread(read(g6.at[1], 2), 3), weights(c6, 2)
-    black = relaxed_spread(gr6, gk6, w6, 1, 3)
-    red = relaxed_spread(black, gr6, w6, 0, 2)
-    black = relaxed_spread(red, gk6, w6, 1, 1)
-    put(k6, black[0])
-    new = relaxed_spread(black, gr6, w6, 0, 0)[0]
-    put(s6, [c6[4, pl.ds(WB + 8 * b, 8), :] * (new[b] - red[0][b]) for b in range(2)])
-    restrict_pass(s6, WB, 1, nat, g7, WB, c7, 0, 1, ((0, 0),))
-    gr7, gk7, w7 = spread(read(g7.at[0], 1), 4), spread(read(g7.at[1], 1), 3), weights(c7, 1)
+    restrict_pass(s5, WB, 2, mix, nat, g6, WB, c6, 0, 2, ((0, 1),))
+    spread_down(k6, g6, s6, c6, WB, 2, 1)
+    restrict_pass(s6, WB, 1, mix, nat, g7, WB, c7, 0, 1, ((0, 0),))
+    gr7, gk7, w7 = spread(read(g7.at[0], WB, 1), 4), spread(read(g7.at[1], WB, 1), 3), weights(c7, WB, 1)
     source = gr7
     for step in range(4):
         black = relaxed_spread(source, gk7, w7, 1, 3 if step < 3 else 2)
@@ -476,8 +531,8 @@
         black = relaxed_spread(red, gk7, w7, 1, 1 if step < 3 else 0)
         if step < 3:
             source = spread(relaxed_spread(black, gr7, w7, 0, 0)[0], 4)
-    put(r7, red[0])
-    put(k7, black[0])
+    put(r7, WB, red[0])
+    put(k7, WB, black[0])
 
     def whole_up(rc, kc, blocks, nc, fine, plan):
         for k in range(blocks):
@@ -485,11 +540,7 @@
         prolong_pass(e_ref, f_ref, fb_ref, 0, 2 * blocks, fine, WB, 0, 2 * blocks, plan, True)
 
     whole_up(r7, k7, 1, 1, k6, ((0, 0),))
-    red = relaxed_spread(spread(read(k6, 2), 4), gr6, w6, 0, 3)
-    black = relaxed_spread(red, gk6, w6, 1, 2)
-    red = relaxed_spread(black, gr6, w6, 0, 1)
-    put(r6, red[0])
-    put(k6, relaxed_spread(red, gk6, w6, 1, 0)[0])
+    spread_post(r6, k6, g6, c6, WB, 2, 1)
     whole_up(r6, k6, 2, 1, k5, ((0, 0), (0, 1)))
     post(r5, k5, g5, c5, WB, 4, 2)
     whole_up(r5, k5, 4, 2, k4, ((0, 0), (0, 1), (1, 0), (1, 1)))
@@ -519,7 +570,7 @@
             x3[q, 1, pl.ds(BASE[3] + 8 * dr, 8), :] = jnp.where(lane < 64, got(dr, 1), got(dr, -1))
     prolong_pass(win, f_ref, fb_ref, -8, 3, k3, BASE[3], -8, 3, ((0, 0), (0, 1)), False)
     clear_outside((k3, g3.at[0], g3.at[1]), 3, 2)
-    post(r3, k3, g3, c3, BASE[3] - 8, 3, 2)
+    spread_post(r3, k3, g3, c3, BASE[3] - 8, 3, 2)
 
     for k in range(2):
         unpair(r3, k3, BASE[3] - 4 + 8 * k, e_ref, FB - 8 + 16 * k, 2)
@@ -560,8 +611,8 @@
             copy.start()
 
     write(0, r, k, sol_hbm)
-    residual_pass(s, r, k, gr, c0, 0, BASE[0], 8, 9, out_tiles=8)
-    residual_pass(b, k, r, gk, c0, 1, BASE[0], 8, 9, out_tiles=8)
+    residual_pass(s, r, k, gr, c0, 0, BASE[0], 8, 9, tiles=range(8))
+    residual_pass(b, k, r, gk, c0, 1, BASE[0], 8, 9, tiles=range(8))
     write(1, s, b, res_hbm)
     wait_bytes(raw, out_sem)
 
@@ -579,13 +630,13 @@
         levels += [vm(2, tiles, pairs + 2 * WB, 128)] + [vm(tiles, pairs + 2 * WB, 128)] * (2 if l == 3 else 3)
     coefficients = [vm(10, r, 128) for r in ROWS[1:]] + [vm(10, pairs + 2 * WB, 128) for pairs, _ in WHOLE]
     buffers = [
-        vm(2, 3, 8, 128), vm(2, 3, 8, 128), vm(4, 3, 8, 128),
+        vm(2, 3, 8, 128), vm(4, 8, 128), vm(2, 3, 8, 128), vm(4, 8, 128),
         vm(2, 32, 128), vm(2, 32, 128), vm(4, 24, 128),
         vm(8, 3, 8, 128), vm(8, 128), vm(NA - 1, 8, 128), vm(2, 4, 8, 128),
     ]
     dma = pltpu.SemaphoreType.DMA
     sems = [dma] * 11
-    natural = [vm(1, 48, 128), vm(5, 96, 128), vm(9, 96, 128), vm(9, 96, 128), vm(4, 64, 128)]
+    natural = [vm(1, 48, 128), vm(5, 96, 128), vm(9, 96, 128), vm(9, 96, 128), vm(9, 64, 128), vm(4, 64, 128)]
     held = (vm(3, 9, ROWS[0], 128), vm(10, ROWS[0], 128))
     inside = pl.BlockSpec(memory_space=pltpu.VMEM)
     outside = pl.BlockSpec(memory_space=pl.ANY)

time: 40.8 us -> 40.1 us (0.983)
  Pallas kernels: 40 us -> 39.2 us
    pallas_call x1, Pallas kernels: 38.1 us -> 37.3 us  [local(): pl.pallas_call(kernel, out_shape=held, in_specs=[outside] * 2, out_specs=...]
where the time goes in v5:
time: 40.1 us; the launch traced here: 39.9 us
  Pallas kernels  39.2 us (98%)
  between operations  0.64 us (2%)
    pallas_call x1, Pallas kernels, local(): pl.pallas_call(kernel, out_shape=held, in_specs=[outside] * 2, out_specs=...  37.3 us
    pallas_call x1, Pallas kernels, local(): pl.pallas_call(finish, out_shape=(block, block), in_specs=[inside] * 2, o...  1.94 us

profile of v5, /device:TPU:1, one launch (start us, length us, event | category | flops | bytes accessed | tf_op | source)
XLA Modules:
  0.0 39.9 jit_solution(10493149023148038095)
XLA Ops:
  0.6 37.3 %shard_map.41 = (f32[3,9,80,128]{3,2,1,0:T(8,128)S(1)}, f32[10,80,128]{2,1,0:T(8,128)S(1)}) custom-call(f32[128,1024]{1,0:T(8,128)} %right_hbm.1, f32[128,1024]{1,0:T(8,128)} %guess_hbm.1), custom_call_target="tpu_custom_call" | custom-call | tf_op jit(solution)/shard_map/pallas_call | solution.py:643
  37.9 1.9 %shard_map.42 = (f32[128,1024]{1,0:T(8,128)}, f32[128,1024]{1,0:T(8,128)}) custom-call(f32[3,9,80,128]{3,2,1,0:T(8,128)S(1)} %get-tuple-element.4.x0, f32[10,80,128]{2,1,0:T(8,128)S(1)} %get-tuple-element.5.c0), custom_call_target="tpu_custom_call" | custom-call | tf_op jit(solution)/shard_map/pallas_call | solution.py:653

commit v6 on v5

--- a/solution.py
+++ b/solution.py
@@ -165,33 +165,33 @@
         dst[t, pl.ds(q + 1, 8, stride=2), :] = jnp.where(even, y, x)
 
 
-def prolong_pass(e, f, fb, start, count, fine, fine_base, fine_start, fine_count, plan, sealed):
+def prolong_pass(e, f, fa, fb, start, count, fine, fine_base, fine_start, fine_count, plan, sealed):
     _, lane = grid_ids()
     even = lane % 2 == 0
     half = lane // 2
+    kinds = (half, half + 64, jnp.where(lane < 64, half, half + 64))
     nc = max(source for source, _ in plan) + 1
-
-    def arranged(x, kind):
-        if kind == 0:
-            return x
-        turned = pltpu.roll(x, 64, 1)
-        return turned if kind == 1 else jnp.where(lane < 32, x, turned)
-
     for k in range(count):
-        p = FB + start + 8 * k
-        x = [e[t, pl.ds(p, 8), :] for t in range(nc)]
+        at = pl.ds(FB + start + 8 * k, 8)
+        x = [e[t, at, :] for t in range(nc)]
         left, right = ring_shift(x, lane)
-        for t, (source, kind) in enumerate(plan):
-            f[t, pl.ds(p, 8), :] = arranged(0.75 * x[source] + 0.25 * left[source], kind)
-            fb[t, pl.ds(p, 8), :] = arranged(0.75 * x[source] + 0.25 * right[source], kind)
-
-    def gathers():
-        for k in range(count):
-            at = pl.ds(FB + start + 8 * k, 8)
-            for t in range(len(plan)):
-                f[t, at, :] = jnp.where(even, pick(f[t, at, :], half), pick(fb[t, at, :], half))
-
-    fence(gathers)
+        for t in range(nc):
+            fa[t, at, :] = 0.75 * x[t] + 0.25 * left[t]
+            fb[t, at, :] = 0.75 * x[t] + 0.25 * right[t]
+
+    for wanted, index in enumerate(kinds):
+        tiles = [(t, source) for t, (source, kind) in enumerate(plan) if kind == wanted]
+
+        def gathers(tiles=tiles, index=index):
+            for k in range(count):
+                at = pl.ds(FB + start + 8 * k, 8)
+                for t, source in tiles:
+                    f[t, at, :] = jnp.where(even, pick(fa[source, at, :], index), pick(fb[source, at, :], index))
+
+        if tiles and wanted < 2:
+            fence(gathers)
+        elif tiles:
+            gathers()
     if sealed:
         for t in range(len(plan)):
             f[t, pl.ds(FB - 8, 8), :] = jnp.zeros((8, 128), F32)
@@ -311,7 +311,7 @@
     right_hbm, guess_hbm, x0, c0,
     raw, r0, s0, g1, r1, k1, s1, g2, r2, k2, s2, x3, r3, s3,
     g4, r4, k4, s4, g5, r5, k5, s5, g6, r6, k6, s6, g7, r7, k7,
-    win, e_ref, f_ref, fb_ref, mix, nat, c1, c2, c3, c4, c5, c6, c7,
+    win, e_ref, f_ref, fa_ref, fb_ref, mix, nat, c1, c2, c3, c4, c5, c6, c7,
     pk0, pc0, rp0, rd0, pk1, rl1, rd1, bs3, own4, slots, strip,
     load_sem, send0, recv0, send1, recv1, sendc, recvc, senda, recva, sendg, recvg,
 ):
@@ -537,7 +537,7 @@
     def whole_up(rc, kc, blocks, nc, fine, plan):
         for k in range(blocks):
             unpair(rc, kc, WB + 8 * k, e_ref, FB + 16 * k, nc)
-        prolong_pass(e_ref, f_ref, fb_ref, 0, 2 * blocks, fine, WB, 0, 2 * blocks, plan, True)
+        prolong_pass(e_ref, f_ref, fa_ref, fb_ref, 0, 2 * blocks, fine, WB, 0, 2 * blocks, plan, True)
 
     whole_up(r7, k7, 1, 1, k6, ((0, 0),))
     spread_post(r6, k6, g6, c6, WB, 2, 1)
@@ -568,26 +568,26 @@
         x3[q, 0, pl.ds(BASE[3] + 8, 8), :] = got(1, 0)
         for dr in (-1, 0, 1):
             x3[q, 1, pl.ds(BASE[3] + 8 * dr, 8), :] = jnp.where(lane < 64, got(dr, 1), got(dr, -1))
-    prolong_pass(win, f_ref, fb_ref, -8, 3, k3, BASE[3], -8, 3, ((0, 0), (0, 1)), False)
+    prolong_pass(win, f_ref, fa_ref, fb_ref, -8, 3, k3, BASE[3], -8, 3, ((0, 0), (0, 1)), False)
     clear_outside((k3, g3.at[0], g3.at[1]), 3, 2)
     spread_post(r3, k3, g3, c3, BASE[3] - 8, 3, 2)
 
     for k in range(2):
         unpair(r3, k3, BASE[3] - 4 + 8 * k, e_ref, FB - 8 + 16 * k, 2)
-    prolong_pass(e_ref, f_ref, fb_ref, -8, 4, k2, BASE[2], -4, 3, ((0, 0), (0, 1), (1, 2)), False)
+    prolong_pass(e_ref, f_ref, fa_ref, fb_ref, -8, 4, k2, BASE[2], -4, 3, ((0, 0), (0, 1), (1, 2)), False)
     clear_outside((k2,), 2, 3)
     post(r2, k2, g2, c2, BASE[2] - 4, 3, 3)
 
     for k in range(3):
         unpair(r2, k2, BASE[2] - 4 + 8 * k, e_ref, FB - 8 + 16 * k, 3)
-    prolong_pass(e_ref, f_ref, fb_ref, -8, 6, k1, BASE[1], -4, 5, ((0, 0), (0, 1), (1, 0), (1, 1), (2, 2)), False)
+    prolong_pass(e_ref, f_ref, fa_ref, fb_ref, -8, 6, k1, BASE[1], -4, 5, ((0, 0), (0, 1), (1, 0), (1, 1), (2, 2)), False)
     clear_outside((k1,), 1, 5)
     post(r1, k1, g1, c1, BASE[1] - 4, 5, 5)
 
     for k in range(5):
         unpair(r1, k1, BASE[1] - 4 + 8 * k, e_ref, FB - 8 + 16 * k, 5)
     plan = tuple((t // 2, t % 2) for t in range(8)) + ((4, 2),)
-    prolong_pass(e_ref, f_ref, fb_ref, -8, 10, k0, BASE[0], -4, 9, plan, False)
+    prolong_pass(e_ref, f_ref, fa_ref, fb_ref, -8, 10, k0, BASE[0], -4, 9, plan, False)
     clear_outside((k0,), 0, 9)
 
 
@@ -636,7 +636,7 @@
     ]
     dma = pltpu.SemaphoreType.DMA
     sems = [dma] * 11
-    natural = [vm(1, 48, 128), vm(5, 96, 128), vm(9, 96, 128), vm(9, 96, 128), vm(9, 64, 128), vm(4, 64, 128)]
+    natural = [vm(1, 48, 128), vm(5, 96, 128), vm(9, 96, 128), vm(5, 96, 128), vm(5, 96, 128), vm(9, 64, 128), vm(4, 64, 128)]
     held = (vm(3, 9, ROWS[0], 128), vm(10, ROWS[0], 128))
     inside = pl.BlockSpec(memory_space=pltpu.VMEM)
     outside = pl.BlockSpec(memory_space=pl.ANY)

time: 40.1 us -> 39.7 us (0.990)
  no operation moved by 1% of the time
where the time goes in v6:
time: 39.7 us; the launch traced here: 39.5 us
  Pallas kernels  38.9 us (98%)
  between operations  0.64 us (2%)
    pallas_call x1, Pallas kernels, local(): pl.pallas_call(kernel, out_shape=held, in_specs=[outside] * 2, out_specs=...  36.9 us
    pallas_call x1, Pallas kernels, local(): pl.pallas_call(finish, out_shape=(block, block), in_specs=[inside] * 2, o...  1.94 us

profile of v6, /device:TPU:1, one launch (start us, length us, event | category | flops | bytes accessed | tf_op | source)
XLA Modules:
  0.0 39.5 jit_solution(3457304439063719142)
XLA Ops:
  0.6 36.9 %shard_map.41 = (f32[3,9,80,128]{3,2,1,0:T(8,128)S(1)}, f32[10,80,128]{2,1,0:T(8,128)S(1)}) custom-call(f32[128,1024]{1,0:T(8,128)} %right_hbm.1, f32[128,1024]{1,0:T(8,128)} %guess_hbm.1), custom_call_target="tpu_custom_call" | custom-call | tf_op jit(solution)/shard_map/pallas_call | solution.py:643
  37.6 1.9 %shard_map.42 = (f32[128,1024]{1,0:T(8,128)}, f32[128,1024]{1,0:T(8,128)}) custom-call(f32[3,9,80,128]{3,2,1,0:T(8,128)S(1)} %get-tuple-element.4.x0, f32[10,80,128]{2,1,0:T(8,128)S(1)} %get-tuple-element.5.c0), custom_call_target="tpu_custom_call" | custom-call | tf_op jit(solution)/shard_map/pallas_call | solution.py:653

commit v7 on v6

--- a/solution.py
+++ b/solution.py
@@ -165,8 +165,11 @@
         dst[t, pl.ds(q + 1, 8, stride=2), :] = jnp.where(even, y, x)
 
 
-def prolong_pass(e, f, fa, fb, start, count, fine, fine_base, fine_start, fine_count, plan, sealed):
-    _, lane = grid_ids()
+def prolong_pass(e, f, fa, fb, start, count, fine, fine_base, fine_start, fine_count, plan, sealed, own=0):
+    sub, lane = grid_ids()
+    me_r = lax.axis_index("rad")
+    low = jnp.where(me_r == 0, 0, -64)
+    high = jnp.where(me_r == NB - 1, own, 1024)
     even = lane % 2 == 0
     half = lane // 2
     kinds = (half, half + 64, jnp.where(lane < 64, half, half + 64))
@@ -201,7 +204,10 @@
         at = pl.ds(fine_base + i, 8)
         for t in range(len(plan)):
             other = jnp.where(even, f[t, pl.ds(FB + i + 1, 8), :], f[t, pl.ds(FB + i - 1, 8), :])
-            fine[t, at, :] = fine[t, at, :] + (0.75 * f[t, pl.ds(FB + i, 8), :] + 0.25 * other)
+            value = fine[t, at, :] + (0.75 * f[t, pl.ds(FB + i, 8), :] + 0.25 * other)
+            if own and k in (0, fine_count - 1):
+                value = jnp.where(jnp.logical_and(i + sub >= low, i + sub < high), value, 0.0)
+            fine[t, at, :] = value
 
 
 def wait_bytes(ref, *sems):
@@ -563,32 +569,29 @@
 
     wait_bytes(bs3, sendc, recvc)
     for q in range(3):
-        got = lambda dr, da: bs3[DIRS.index((-dr, -da)), q]
+        keep = {-1: jnp.where(me_r == 0, 0.0, 1.0), 0: 1.0, 1: jnp.where(me_r == NB - 1, 0.0, 1.0)}
+        got = lambda dr, da: bs3[DIRS.index((-dr, -da)), q] * keep[dr]
         x3[q, 0, pl.ds(BASE[3] - 8, 8), :] = got(-1, 0)
         x3[q, 0, pl.ds(BASE[3] + 8, 8), :] = got(1, 0)
         for dr in (-1, 0, 1):
             x3[q, 1, pl.ds(BASE[3] + 8 * dr, 8), :] = jnp.where(lane < 64, got(dr, 1), got(dr, -1))
-    prolong_pass(win, f_ref, fa_ref, fb_ref, -8, 3, k3, BASE[3], -8, 3, ((0, 0), (0, 1)), False)
-    clear_outside((k3, g3.at[0], g3.at[1]), 3, 2)
+    prolong_pass(win, f_ref, fa_ref, fb_ref, -8, 3, k3, BASE[3], -8, 3, ((0, 0), (0, 1)), False, OWN[3][0])
     spread_post(r3, k3, g3, c3, BASE[3] - 8, 3, 2)
 
     for k in range(2):
         unpair(r3, k3, BASE[3] - 4 + 8 * k, e_ref, FB - 8 + 16 * k, 2)
-    prolong_pass(e_ref, f_ref, fa_ref, fb_ref, -8, 4, k2, BASE[2], -4, 3, ((0, 0), (0, 1), (1, 2)), False)
-    clear_outside((k2,), 2, 3)
+    prolong_pass(e_ref, f_ref, fa_ref, fb_ref, -8, 4, k2, BASE[2], -4, 3, ((0, 0), (0, 1), (1, 2)), False, OWN[2][0])
     post(r2, k2, g2, c2, BASE[2] - 4, 3, 3)
 
     for k in range(3):
         unpair(r2, k2, BASE[2] - 4 + 8 * k, e_ref, FB - 8 + 16 * k, 3)
-    prolong_pass(e_ref, f_ref, fa_ref, fb_ref, -8, 6, k1, BASE[1], -4, 5, ((0, 0), (0, 1), (1, 0), (1, 1), (2, 2)), False)
-    clear_outside((k1,), 1, 5)
+    prolong_pass(e_ref, f_ref, fa_ref, fb_ref, -8, 6, k1, BASE[1], -4, 5, ((0, 0), (0, 1), (1, 0), (1, 1), (2, 2)), False, OWN[1][0])
     post(r1, k1, g1, c1, BASE[1] - 4, 5, 5)
 
     for k in range(5):
         unpair(r1, k1, BASE[1] - 4 + 8 * k, e_ref, FB - 8 + 16 * k, 5)
     plan = tuple((t // 2, t % 2) for t in range(8)) + ((4, 2),)
-    prolong_pass(e_ref, f_ref, fa_ref, fb_ref, -8, 10, k0, BASE[0], -4, 9, plan, False)
-    clear_outside((k0,), 0, 9)
+    prolong_pass(e_ref, f_ref, fa_ref, fb_ref, -8, 10, k0, BASE[0], -4, 9, plan, False, OWN[0][0])
 
 
 def finish(x0, c0, sol_hbm, res_hbm, r, k, s, b, raw, out_sem):

time: 39.7 us -> 39.7 us (level)
  no operation moved by 1% of the time
where the time goes in v7:
time: 39.7 us; the launch traced here: 39.5 us
  Pallas kernels  38.9 us (98%)
  between operations  0.64 us (2%)
    pallas_call x1, Pallas kernels, local(): pl.pallas_call(kernel, out_shape=held, in_specs=[outside] * 2, out_specs=...  36.9 us
    pallas_call x1, Pallas kernels, local(): pl.pallas_call(finish, out_shape=(block, block), in_specs=[inside] * 2, o...  1.94 us

profile of v7, /device:TPU:1, one launch (start us, length us, event | category | flops | bytes accessed | tf_op | source)
XLA Modules:
  0.0 39.5 jit_solution(15489325270389013566)
XLA Ops:
  0.6 36.9 %shard_map.41 = (f32[3,9,80,128]{3,2,1,0:T(8,128)S(1)}, f32[10,80,128]{2,1,0:T(8,128)S(1)}) custom-call(f32[128,1024]{1,0:T(8,128)} %right_hbm.1, f32[128,1024]{1,0:T(8,128)} %guess_hbm.1), custom_call_target="tpu_custom_call" | custom-call | tf_op jit(solution)/shard_map/pallas_call | solution.py:646
  37.6 1.9 %shard_map.42 = (f32[128,1024]{1,0:T(8,128)}, f32[128,1024]{1,0:T(8,128)}) custom-call(f32[3,9,80,128]{3,2,1,0:T(8,128)S(1)} %get-tuple-element.4.x0, f32[10,80,128]{2,1,0:T(8,128)S(1)} %get-tuple-element.5.c0), custom_call_target="tpu_custom_call" | custom-call | tf_op jit(solution)/shard_map/pallas_call | solution.py:656

commit v8 on v7

--- a/solution.py
+++ b/solution.py
@@ -426,16 +426,16 @@
             send(pc0.at[c, pl.ds(0 if dr < 0 else 8 - E0, E0), :], rd0.at[c, pl.ds(0, E0), :], send0, recv0, dr, da)
     wait_bytes(f_ref.at[pl.ds(0, 4), pl.ds(0, 69), :], send0, recv0)
 
+    keep_before = jnp.where(me_r == 0, 0.0, 1.0)
+    keep_after = jnp.where(me_r == NB - 1, 0.0, 1.0)
+
     def clear_outside(refs, l, n, depth=1):
-        @pl.when(me_r == 0)
-        def _():
-            for ref in refs:
-                zero_rows(ref, n, BASE[l] - 8 * depth, depth)
-
-        @pl.when(me_r == NB - 1)
-        def _():
-            for ref in refs:
-                zero_rows(ref, n, BASE[l] + OWN[l][0], depth)
+        for ref in refs:
+            for t in range(n):
+                for d in range(depth):
+                    before, after = pl.ds(BASE[l] - 8 * (d + 1), 8), pl.ds(BASE[l] + OWN[l][0] + 8 * d, 8)
+                    ref[t, before, :] = ref[t, before, :] * keep_before
+                    ref[t, after, :] = ref[t, after, :] * keep_after
 
     for q in range(3):
         from_left, from_right = rp0[1, q], rp0[0, q]

time: 39.7 us -> 39.6 us (level)
  no operation moved by 1% of the time
where the time goes in v8:
time: 39.6 us; the launch traced here: 39.4 us
  Pallas kernels  38.8 us (98%)
  between operations  0.64 us (2%)
    pallas_call x1, Pallas kernels, local(): pl.pallas_call(kernel, out_shape=held, in_specs=[outside] * 2, out_specs=...  36.8 us
    pallas_call x1, Pallas kernels, local(): pl.pallas_call(finish, out_shape=(block, block), in_specs=[inside] * 2, o...  1.94 us

profile of v8, /device:TPU:1, one launch (start us, length us, event | category | flops | bytes accessed | tf_op | source)
XLA Modules:
  0.0 39.4 jit_solution(17092544266618992300)
XLA Ops:
  0.6 36.8 %shard_map.41 = (f32[3,9,80,128]{3,2,1,0:T(8,128)S(1)}, f32[10,80,128]{2,1,0:T(8,128)S(1)}) custom-call(f32[128,1024]{1,0:T(8,128)} %right_hbm.1, f32[128,1024]{1,0:T(8,128)} %guess_hbm.1), custom_call_target="tpu_custom_call" | custom-call | tf_op jit(solution)/shard_map/pallas_call | solution.py:646
  37.5 1.9 %shard_map.42 = (f32[128,1024]{1,0:T(8,128)}, f32[128,1024]{1,0:T(8,128)}) custom-call(f32[3,9,80,128]{3,2,1,0:T(8,128)S(1)} %get-tuple-element.4.x0, f32[10,80,128]{2,1,0:T(8,128)S(1)} %get-tuple-element.5.c0), custom_call_target="tpu_custom_call" | custom-call | tf_op jit(solution)/shard_map/pallas_call | solution.py:656
